TPU v7x, 512 devices: a whole 4x8x8 slice. The times are simulated.
512 devices in a mesh: dp: 32 (over x, y), tensor: 16 (over z, core).
Axes of the slice: x: 4, y: 8, z: 8, core: 2. Of those that a mesh axis runs over, the one named last changes fastest.
Arguments:
- queries: bfloat16 [4096, 16384], P('dp', 'tensor'), may hold values from -24 to 24
- draft_keys: bfloat16 [4096, 1024], P('dp'), may hold values from -6 to 6
- draft_values: bfloat16 [4096, 1024], P('dp'), may hold values from -6 to 6
- cache_keys: bfloat16 [64, 2048, 1024], P('dp', 'tensor'), may hold values from -24 to 24
- cache_values: bfloat16 [64, 2048, 1024], P('dp', 'tensor'), may hold values from -6 to 6
- out_weight: bfloat16 [16384, 16384], P('tensor', 'dp'), may hold values from -0.25 to 0.25
- cache_lengths: int32 [64], P('dp'), may hold values from 512 to 2048
- draft_lengths: int32 [64], replicated, may hold values from 8 to 64
- dest_group: int32 [64], replicated, may hold values from 0 to 31, as said below
- dest_offset: int32 [64], replicated, may hold values from 0 to 32, as said below
Outputs:
- verified: bfloat16 [3072, 16384], P('tensor', 'dp')
Inputs may be any that keep to these rules, and one draw needn't show every extreme that they name: `dest_group`: at most one request of a group has another group as destination, and each group receives at most one such request. `dest_offset`: blocks with the same destination never intersect and end at packed row 96 or before; a block moved to another group starts right after that group's own rows; in every draw some group's blocks fill all 96 rows.
All inputs are finite; a program needn't handle non-finite values.
Results may differ from a plain program's by a relative error of at most 0.017.
Values may be sent and summed in bfloat16 or wider, within the bound.
No kernel may reach another device: no remote copies, remote signals or barrier semaphores. Data moves between devices by JAX's collectives and lax.ppermute only.
A program may use at most 64 MiB of HBM per device.

v0:
```python
import jax
import jax.numpy as jnp
from jax import lax
from jax.experimental import pallas as pl
from jax.experimental.pallas import tpu as pltpu
from jax.sharding import Mesh, PartitionSpec as P


HEAD_DIM = 128
DRAFT = 64
PACK = 96
NX, NY, NZ = 4, 8, 8
NEG_FILL = -1e30
EXP2_SCALE = HEAD_DIM ** (-0.5) * 1.4426950408889634
BF16 = jnp.bfloat16
F32 = jnp.float32
NT = (((1,), (1,)), ((), ()))
VMEM = pl.BlockSpec(memory_space=pltpu.VMEM)
SMEM = pl.BlockSpec(memory_space=pltpu.SMEM)
PARAMS = pltpu.CompilerParams(vmem_limit_bytes=24 * 2**20)

CHUNKS = ((0, -1, 1, -2, 2), (-3, 3, -4))


def shift(value, axis, size, step):
    return lax.ppermute(value, axis, [(i, (i + step) % size) for i in range(size)])


def shift_cores(value, axis, size, step):
    pairs = [(2 * i + c, 2 * ((i + step * (1 - 2 * c)) % size) + c) for i in range(size) for c in (0, 1)]
    return lax.ppermute(value, (axis, "c"), pairs)


def near(value):
    return pltpu.with_memory_space_constraint(value, pltpu.VMEM)


def kv_kernel(k_ref, v_ref, o_ref):
    for h in range(NZ):
        o_ref[h, 0, 0] = k_ref[0, :, h * HEAD_DIM : (h + 1) * HEAD_DIM]
        o_ref[h, 0, 1] = v_ref[0, :, h * HEAD_DIM : (h + 1) * HEAD_DIM]


def pack_kv(k, v):
    return pl.pallas_call(
        kv_kernel,
        grid=(2,),
        in_specs=[pl.BlockSpec((1, 128, 1024), lambda r: (r, 0, 0))] * 2,
        out_specs=pl.BlockSpec((NZ, 1, 2, 128, 128), lambda r: (0, r, 0, 0, 0)),
        out_shape=pltpu.VMEM((NZ, 2, 2, 128, 128), BF16),
        compiler_params=PARAMS,
        name="pack_kv",
    )(k, v)


def attend_kernel(s_ref, cache_ref, draft_ref, mine_ref, other_ref, kv_ref, dk_ref, dv_ref, o_ref):
    cache_len = cache_ref[s_ref[3]]
    draft_len = draft_ref[(s_ref[0] * NY + s_ref[1]) * 2 + s_ref[3]]
    keys = kv_ref[:, 0].reshape(2048, HEAD_DIM)
    values = kv_ref[:, 1].reshape(2048, HEAD_DIM)
    dk = dk_ref[...]
    dv = dv_ref[...]
    keep = lax.broadcasted_iota(jnp.int32, (1, 2048), 1) < cache_len
    row = lax.broadcasted_iota(jnp.int32, (256, DRAFT), 0) % DRAFT
    slot = lax.broadcasted_iota(jnp.int32, (256, DRAFT), 1)
    keep_draft = (slot <= row) & (slot < draft_len)
    live = lax.broadcasted_iota(jnp.int32, (256, 1), 0) % DRAFT < draft_len
    for side, q_ref in enumerate((mine_ref, other_ref)):
        q = jnp.concatenate([q_ref[:, h * HEAD_DIM : (h + 1) * HEAD_DIM] for h in range(4)], axis=0)
        cached = lax.dot_general(q, keys, NT, preferred_element_type=F32)
        drafted = lax.dot_general(q, dk, NT, preferred_element_type=F32)
        cached = jnp.where(keep, cached, NEG_FILL)
        drafted = jnp.where(keep_draft, drafted, NEG_FILL)
        high = jnp.maximum(
            jnp.max(cached, axis=1, keepdims=True), jnp.max(drafted, axis=1, keepdims=True)
        )
        cached = jnp.exp2((cached - high) * EXP2_SCALE)
        drafted = jnp.exp2((drafted - high) * EXP2_SCALE)
        total = jnp.sum(cached, axis=1, keepdims=True) + jnp.sum(drafted, axis=1, keepdims=True)
        mixed = jnp.dot(cached.astype(BF16), values, preferred_element_type=F32)
        mixed = mixed + jnp.dot(drafted.astype(BF16), dv, preferred_element_type=F32)
        mixed = jnp.where(live, mixed / total, 0.0).astype(BF16)
        for h in range(4):
            o_ref[side, :, h * HEAD_DIM : (h + 1) * HEAD_DIM] = mixed[h * DRAFT : (h + 1) * DRAFT]


def attend(ids, cache_lengths, draft_lengths, q, other_q, kv, dk, dv):
    draft = pl.BlockSpec((DRAFT, HEAD_DIM), lambda p, s, *_: (s[3], s[2]))
    return pl.pallas_call(
        attend_kernel,
        grid_spec=pltpu.PrefetchScalarGridSpec(
            num_scalar_prefetch=3,
            grid=(2,),
            in_specs=[
                pl.BlockSpec((DRAFT, 512), lambda p, s, *_: (s[3], p)),
                pl.BlockSpec((DRAFT, 512), lambda p, *_: (0, p)),
                pl.BlockSpec((16, 2, 128, 128), lambda p, *_: (0, 0, 0, 0)),
                draft,
                draft,
            ],
            out_specs=pl.BlockSpec((2, DRAFT, 512), lambda p, *_: (0, 0, p)),
        ),
        out_shape=pltpu.VMEM((2, DRAFT, 1024), BF16),
        compiler_params=PARAMS,
        name="attend",
    )(ids, cache_lengths, draft_lengths, q, other_q, kv, dk, dv)


def project_kernel(count, s_ref, *refs):
    rows, weights, o_ref = refs[:count], refs[count:-1], refs[-1]
    width = count * DRAFT
    a = jnp.concatenate([ref[0] for ref in rows], axis=0)
    b = jnp.concatenate([ref[1] for ref in rows], axis=0)
    for i, step in enumerate((0, -1, 1, 2)):
        acc = jnp.dot(a, weights[2 * i][...], preferred_element_type=F32)
        acc = acc + jnp.dot(b, weights[2 * i + 1][...], preferred_element_type=F32)
        acc = acc.astype(BF16).T.reshape(NZ, 2, 32, width)
        at = lax.rem(s_ref[0] + step + NX, NX)
        for half in range(2):
            o_ref[at, :, :, half * width : (half + 1) * width] = acc[:, half]


def project(ids, rows, weights):
    count = len(rows)
    return pl.pallas_call(
        lambda *refs: project_kernel(count, *refs),
        in_specs=[SMEM] + [VMEM] * (count + 8),
        out_specs=VMEM,
        out_shape=pltpu.VMEM((NX, NZ, 32, 2 * count * DRAFT), BF16),
        compiler_params=PARAMS,
        name="project",
    )(ids, *map(near, rows), *map(near, weights))


def place_kernel(s_ref, length_ref, group_ref, first_ref, *refs):
    parts, o_ref, f_ref = refs[:-2], refs[-2], refs[-1]
    f_ref[...] = jnp.zeros(f_ref.shape, F32)
    my_y, core = s_ref[1], s_ref[3]
    lane = lax.broadcasted_iota(jnp.int32, (32, 128), 1)
    for x in range(NX):
        for slots, ref in zip(CHUNKS, parts):
            width = len(slots) * DRAFT
            for tile in range(2 * width // 128):
                slab = ref[x, 0, :, tile * 128 : (tile + 1) * 128].astype(F32)
                for z in range(1, NZ):
                    slab = slab + ref[x, z, :, tile * 128 : (tile + 1) * 128].astype(F32)
                for part in range(2):
                    column, at = divmod(2 * tile + part, len(slots))
                    request = (x * NY + lax.rem(my_y + slots[at] + NY, NY)) * 2 + core
                    length, group, first = length_ref[request], group_ref[request], first_ref[request]
                    moved = pltpu.roll(slab, lax.rem(first + 64 * part, 128), 1)
                    keep = (lane >= first) & (lane < first + length)
                    spot = 2 * group + column
                    f_ref[spot] = f_ref[spot] + jnp.where(keep, moved, 0.0)
    for t in range(16):
        a, b, c, d = (f_ref[4 * t + i] for i in range(4))
        b, c, d = pltpu.roll(b, 96, 1), pltpu.roll(c, 64, 1), pltpu.roll(d, 32, 1)
        o_ref[t, :, :128] = jnp.where(lane < 96, a, b).astype(BF16)
        o_ref[t, :, 128:256] = jnp.where(lane < 64, b, c).astype(BF16)
        o_ref[t, :, 256:] = jnp.where(lane < 32, c, d).astype(BF16)


def place(tables, parts):
    return pl.pallas_call(
        place_kernel,
        in_specs=[SMEM] * len(tables) + [VMEM] * len(parts),
        out_specs=VMEM,
        out_shape=pltpu.VMEM((16, 32, 4 * PACK), BF16),
        scratch_shapes=[pltpu.VMEM((64, 32, 128), F32)],
        compiler_params=PARAMS,
        name="place",
    )(*tables, *map(near, parts))


def finish_kernel(i_ref, o_ref):
    lane = lax.broadcasted_iota(jnp.int32, (32, 128), 1)
    blocks = [[], []]
    for z in range(NZ):
        v = i_ref[2 * z].astype(F32) + i_ref[2 * z + 1].astype(F32)
        v = [v[:, i * 128 : (i + 1) * 128] for i in range(3)]
        blocks[0].append(v[0])
        blocks[0].append(pltpu.roll(jnp.where(lane < 64, v[1], v[0]), 32, 1))
        blocks[1].append(pltpu.roll(jnp.where(lane < 32, v[2], v[1]), 64, 1))
        blocks[1].append(pltpu.roll(v[2], 96, 1))
    for g in range(2):
        block = jnp.concatenate(blocks[g], axis=0).astype(BF16).T
        o_ref[g * PACK : (g + 1) * PACK] = block[:PACK]


def finish(parts):
    return pl.pallas_call(
        finish_kernel,
        in_specs=[VMEM],
        out_specs=VMEM,
        out_shape=jax.ShapeDtypeStruct((2 * PACK, 512), BF16),
        compiler_params=PARAMS,
        name="finish",
    )(near(parts))


def exchange(value, axes):
    return lax.all_to_all(value, axes, 0, 0, tiled=True)


def layer(
    queries,
    draft_keys,
    draft_values,
    cache_keys,
    cache_values,
    out_weight,
    cache_lengths,
    draft_lengths,
    dest_group,
    dest_offset,
):
    c = lax.axis_index("c")
    ids = jnp.stack([lax.axis_index(name) for name in ("x", "y", "z", "c")]).astype(jnp.int32)

    kv = exchange(pack_kv(cache_keys, cache_values).reshape(16, 2, 128, 128), ("z", "c"))

    w1, w2 = shift(out_weight, "x", NX, 1), shift(out_weight, "x", NX, -1)
    w3 = shift_cores(out_weight, "x", NX, 2)
    weights = []
    for w in (out_weight, w1, w2, w3):
        weights += [w, shift(w, "c", 2, 1)]
    other_q = lax.dynamic_slice_in_dim(queries, (1 - c) * DRAFT, DRAFT, 0)
    other_q = shift(other_q, "c", 2, 1)

    rows = attend(ids, cache_lengths, draft_lengths, queries, other_q, kv, draft_keys, draft_values)
    up1, down1 = shift(rows, "y", NY, 1), shift(rows, "y", NY, -1)
    up2, down2 = shift(up1, "y", NY, 1), shift(down1, "y", NY, -1)
    up3, down3 = shift(up2, "y", NY, 1), shift(down2, "y", NY, -1)
    far = shift_cores(jnp.where(c == 0, up3, down3), "y", NY, 1)
    arrived = {0: rows, -1: up1, 1: down1, -2: up2, 2: down2, -3: up3, 3: down3, -4: far}

    sums = []
    for slots in CHUNKS:
        part = project(ids, [arrived[s] for s in slots], weights)
        part = part.reshape(NX * NZ, 32, -1)
        sums.append(exchange(part, ("x", "z")).reshape(NX, NZ, 32, -1))
    placed = place([ids, draft_lengths, dest_group, dest_offset], sums)
    return finish(exchange(placed, ("z", "c")))


def solution(mesh):
    fine = Mesh(mesh.devices.reshape(NX, NY, NZ, 2), ("x", "y", "z", "c"))
    xy, zc = ("x", "y"), ("z", "c")
    in_specs = (
        P(xy, zc),
        P(xy, None),
        P(xy, None),
        P(xy, zc, None),
        P(xy, zc, None),
        P(zc, xy),
        P(xy),
        P(),
        P(),
        P(),
    )
    return jax.shard_map(layer, mesh=fine, in_specs=in_specs, out_specs=P(zc, xy), check_vma=False)
```

profile of v0, /device:TPU:25, one launch (start us, length us, event | category | flops | bytes accessed | tf_op | source)
XLA Modules:
  0.0 202.6 jit_solution(16622244548738627766)
XLA Ops:
  0.0 1.0 copy-done.7
  1.0 1.0 copy-done.8
  2.1 1.1 pack_kv.1
  3.2 11.1 %all-to-all-start = ((bf16[16,2,128,128]{3,2,1,0:T(8,128)(2,1)}), bf16[16,2,128,128]{3,2,1,0:T(8,128)(2,1)S(1)}, u32[]{:S(2)}, u32[]{:S(2)}) async-start(bf16[16,2,128,128]{3,2,1,0:T(8,128)(2,1)} %bitcast.4), calls=%async_computation | async-start | bytes 2097152 | tf_op jit(solution)/shard_map/all_to_all | solution.py:202
  14.3 3.1 %collective-permute-start.6 = (bf16[1024,512]{1,0:T(8,128)(2,1)S(1)}, bf16[1024,512]{1,0:T(8,128)(2,1)S(1)}, u32[]{:S(2)}, u32[]{:S(2)}) collective-permute-start(bf16[1024,512]{1,0:T(8,128)(2,1)S(1)} %copy-done), channel_id=1, source_target_pairs={{0,128},{128,256},{256,384},{384,0},{1,129},{129,257},{257,385},{3... | collective-permute-start | bytes 3145736 | tf_op jit(solution)/shard_map/ppermute | solution.py:26
  17.5 3.4 %collective-permute-start.8 = (bf16[1024,512]{1,0:T(8,128)(2,1)S(1)}, bf16[1024,512]{1,0:T(8,128)(2,1)}, u32[]{:S(2)}, u32[]{:S(2)}) collective-permute-start(bf16[1024,512]{1,0:T(8,128)(2,1)S(1)} %copy-done), channel_id=1, source_target_pairs={{0,384},{128,0},{256,128},{384,256},{1,385},{129,1},{257,129},{385... | collective-permute-start | bytes 3145736 | tf_op jit(solution)/shard_map/ppermute | solution.py:26
  20.8 3.4 %collective-permute-start.10 = (bf16[1024,512]{1,0:T(8,128)(2,1)S(1)}, bf16[1024,512]{1,0:T(8,128)(2,1)}, u32[]{:S(2)}, u32[]{:S(2)}) collective-permute-start(bf16[1024,512]{1,0:T(8,128)(2,1)S(1)} %copy-done), channel_id=1, source_target_pairs={{0,256},{1,257},{128,384},{129,385},{256,0},{257,1},{384,128},{385... | collective-permute-start | bytes 3145736 | tf_op jit(solution)/shard_map/ppermute | solution.py:31
  24.3 0.7 constant_dynamic-slice_fusion
  25.0 2.8 %collective-permute-start = (bf16[64,1024]{1,0:T(8,128)(2,1)}, bf16[64,1024]{1,0:T(8,128)(2,1)S(1)}, u32[]{:S(2)}, u32[]{:S(2)}) collective-permute-start(bf16[64,1024]{1,0:T(8,128)(2,1)} %constant_dynamic-slice_fusion), channel_id=1, source_target_pairs={{0,1},{1,0},{2,3},{3,2},{4,5},{5,4},{6,7},{7,6},{8,9},{9,8},{10,11... | collective-permute-start | bytes 393224 | tf_op jit(solution)/shard_map/ppermute | solution.py:26
  27.9 1.1 collective-permute-done.other_ref
  29.0 13.3 %all-to-all-done.kv_ref = bf16[16,2,128,128]{3,2,1,0:T(8,128)(2,1)S(1)} async-done(((bf16[16,2,128,128]{3,2,1,0:T(8,128)(2,1)}), bf16[16,2,128,128]{3,2,1,0:T(8,128)(2,1)S(1)}, u32[]{:S(2)}, u32[]{:S(2)}) %all-to-all-start) | async-done | bytes 1048608 | tf_op jit(solution)/shard_map/all_to_all | solution.py:202
  42.3 0.9 copy-done.9
  43.3 0.9 copy-done.10
  44.2 5.1 %attend.1.refs_1_ = bf16[2,64,1024]{2,1,0:T(8,128)(2,1)S(1)} custom-call(s32[4]{0:T(128)S(1)} %pad_add_fusion.s_ref.refs_0_, s32[2]{0:T(128)S(1)} %copy-done.18, s32[64]{0:T(128)S(1)} %copy-done.17, bf16[128,1024]{1,0:T(8,128)(2,1)S(1)} %copy-done.6, bf16[64,1024]{1,0:T(8,128)(2,1)S(1)} %collective-permute-done.other_ref, ...), custom_call_target="tpu_custom_call" | custom-call | tf_op jit(solution)/shard_map/attend/pallas_call | solution.py:89
  49.3 4.4 %collective-permute-start.1 = (bf16[2,64,1024]{2,1,0:T(8,128)(2,1)S(1)}, bf16[2,64,1024]{2,1,0:T(8,128)(2,1)S(1)}, u32[]{:S(2)}, u32[]{:S(2)}) collective-permute-start(bf16[2,64,1024]{2,1,0:T(8,128)(2,1)S(1)} %attend.1.refs_1_), channel_id=1, source_target_pairs={{0,16},{16,32},{32,48},{48,64},{64,80},{80,96},{96,112},{112,0},{1... | collective-permute-start | bytes 786440 | tf_op jit(solution)/shard_map/ppermute | solution.py:26
  53.7 1.9 collective-permute-start.2
  55.7 0.7 copy-done.4
  56.4 2.5 %collective-permute-done.1.refs_2_ = bf16[2,64,1024]{2,1,0:T(8,128)(2,1)S(1)} collective-permute-done((bf16[2,64,1024]{2,1,0:T(8,128)(2,1)S(1)}, bf16[2,64,1024]{2,1,0:T(8,128)(2,1)S(1)}, u32[]{:S(2)}, u32[]{:S(2)}) %collective-permute-start.1) | collective-permute-done | bytes 262176 | tf_op jit(solution)/shard_map/ppermute | solution.py:26
  58.9 5.4 %collective-permute-start.3 = (bf16[2,64,1024]{2,1,0:T(8,128)(2,1)S(1)}, bf16[2,64,1024]{2,1,0:T(8,128)(2,1)S(1)}, u32[]{:S(2)}, u32[]{:S(2)}) collective-permute-start(bf16[2,64,1024]{2,1,0:T(8,128)(2,1)S(1)} %collective-permute-done.1.refs_2_), channel_id=1, source_target_pairs={{0,16},{16,32},{32,48},{48,64},{64,80},{80,96},{96,112},{112,0},{1... | collective-permute-start | bytes 786440 | tf_op jit(solution)/shard_map/ppermute | solution.py:26
  64.3 0.7 copy-done.11
  65.0 1.9 collective-permute-start.4
  67.0 0.7 copy-done.13
  67.7 1.9 collective-permute-start.5
  69.6 2.4 %collective-permute-start.7 = (bf16[1024,512]{1,0:T(8,128)(2,1)S(1)}, bf16[1024,512]{1,0:T(8,128)(2,1)}, u32[]{:S(2)}, u32[]{:S(2)}) collective-permute-start(bf16[1024,512]{1,0:T(8,128)(2,1)S(1)} %collective-permute-done.6.refs_8_.refs_6_), channel_id=1, source_target_pairs={{0,1},{1,0},{2,3},{3,2},{4,5},{5,4},{6,7},{7,6},{8,9},{9,8},{10,11... | collective-permute-start | bytes 3145736 | tf_op jit(solution)/shard_map/ppermute | solution.py:26
  72.0 1.9 collective-permute-start.9
  74.0 2.4 %collective-permute-start.11 = (bf16[1024,512]{1,0:T(8,128)(2,1)}, bf16[1024,512]{1,0:T(8,128)(2,1)}, u32[]{:S(2)}, u32[]{:S(2)}) collective-permute-start(bf16[1024,512]{1,0:T(8,128)(2,1)} %collective-permute-done.10.refs_12_.refs_10_), channel_id=1, source_target_pairs={{0,1},{1,0},{2,3},{3,2},{4,5},{5,4},{6,7},{7,6},{8,9},{9,8},{10,11... | collective-permute-start | bytes 3145736 | tf_op jit(solution)/shard_map/ppermute | solution.py:26
  76.5 4.5 %collective-permute-start.12 = (bf16[2,64,1024]{2,1,0:T(8,128)(2,1)S(1)}, bf16[2,64,1024]{2,1,0:T(8,128)(2,1)S(1)}, u32[]{:S(2)}, u32[]{:S(2)}) collective-permute-start(bf16[2,64,1024]{2,1,0:T(8,128)(2,1)S(1)} %collective-permute-done.3.refs_4_), channel_id=1, source_target_pairs={{0,16},{16,32},{32,48},{48,64},{64,80},{80,96},{96,112},{112,0},{1... | collective-permute-start | bytes 786440 | tf_op jit(solution)/shard_map/ppermute | solution.py:26
  81.0 0.7 copy-done.15
  81.7 4.9 %collective-permute-done.12.refs_1_ = bf16[2,64,1024]{2,1,0:T(8,128)(2,1)S(1)} collective-permute-done((bf16[2,64,1024]{2,1,0:T(8,128)(2,1)S(1)}, bf16[2,64,1024]{2,1,0:T(8,128)(2,1)S(1)}, u32[]{:S(2)}, u32[]{:S(2)}) %collective-permute-start.12) | collective-permute-done | bytes 262176 | tf_op jit(solution)/shard_map/ppermute | solution.py:26
  86.6 1.9 collective-permute-start.13
  88.5 9.5 %collective-permute-done.13.refs_2_ = bf16[2,64,1024]{2,1,0:T(8,128)(2,1)} collective-permute-done((bf16[2,64,1024]{2,1,0:T(8,128)(2,1)}, bf16[2,64,1024]{2,1,0:T(8,128)(2,1)}, u32[]{:S(2)}, u32[]{:S(2)}) %collective-permute-start.13) | collective-permute-done | bytes 262176 | tf_op jit(solution)/shard_map/ppermute | solution.py:26
  98.0 1.0 broadcast_select_fusion
  99.0 1.9 collective-permute-start.14
  101.0 6.3 %collective-permute-done.14.refs_3_ = bf16[2,64,1024]{2,1,0:T(8,128)(2,1)S(1)} collective-permute-done((bf16[2,64,1024]{2,1,0:T(8,128)(2,1)S(1)}, bf16[2,64,1024]{2,1,0:T(8,128)(2,1)S(1)}, u32[]{:S(2)}, u32[]{:S(2)}) %collective-permute-start.14) | collective-permute-done | bytes 262176 | tf_op jit(solution)/shard_map/ppermute | solution.py:31
  107.4 4.6 %project.3 = bf16[4,8,32,384]{3,2,1,0:T(8,128)(2,1)S(1)} custom-call(s32[4]{0:T(128)S(1)} %pad_add_fusion.s_ref.refs_0_, bf16[2,64,1024]{2,1,0:T(8,128)(2,1)S(1)} %collective-permute-done.12.refs_1_, bf16[2,64,1024]{2,1,0:T(8,128)(2,1)} %collective-permute-done.13.refs_2_, bf16[2,64,1024]{2,1,0:T(8,128)(2,1)S(1)} %collective-permute-done.14.refs_3_, ...), custom_call_target="tpu_custom_call" | custom-call | tf_op jit(solution)/shard_map/project/pallas_call | solution.py:125
  111.9 0.9 copy-done.3
  112.9 6.2 %all-to-all-start.2 = ((bf16[32,32,384]{2,1,0:T(8,128)(2,1)}), bf16[32,32,384]{2,1,0:T(8,128)(2,1)}, u32[]{:S(2)}, u32[]{:S(2)}) async-start(bf16[32,32,384]{2,1,0:T(8,128)(2,1)} %bitcast.11), calls=%async_computation.2 | async-start | bytes 1572864 | tf_op jit(solution)/shard_map/all_to_all | solution.py:202
  119.1 1.2 copy-done.2
  120.3 0.9 copy-done.5
  121.2 0.9 copy-done.12
  122.2 0.9 copy-done.14
  123.1 0.9 copy-done.16
  124.1 5.6 %project.2 = bf16[4,8,32,640]{3,2,1,0:T(8,128)(2,1)S(1)} custom-call(s32[4]{0:T(128)S(1)} %pad_add_fusion.s_ref.refs_0_, bf16[2,64,1024]{2,1,0:T(8,128)(2,1)S(1)} %copy-done.5, bf16[2,64,1024]{2,1,0:T(8,128)(2,1)S(1)} %copy-done.12, bf16[2,64,1024]{2,1,0:T(8,128)(2,1)S(1)} %copy-done.14, bf16[2,64,1024]{2,1,0:T(8,128)(2,1)S(1)} %copy-done.16, ...), custom_call_target="tpu_custom_call" | custom-call | tf_op jit(solution)/shard_map/project/pallas_call | solution.py:125
  129.7 8.9 %all-to-all-done.2 = bf16[32,32,384]{2,1,0:T(8,128)(2,1)} async-done(((bf16[32,32,384]{2,1,0:T(8,128)(2,1)}), bf16[32,32,384]{2,1,0:T(8,128)(2,1)}, u32[]{:S(2)}, u32[]{:S(2)}) %all-to-all-start.2) | async-done | bytes 786464 | tf_op jit(solution)/shard_map/all_to_all | solution.py:202
  138.7 39.2 %all_to_all.20 = bf16[32,32,640]{2,1,0:T(8,128)(2,1)S(1)} all-to-all(bf16[32,32,640]{2,1,0:T(8,128)(2,1)S(1)} %bitcast.10), channel_id=1, replica_groups=mesh['x'=4,'y'=8,'z'=8,'c'=2] {'x','z'}, dimensions={0} | all-to-all | bytes 2621440 | tf_op jit(solution)/shard_map/all_to_all | solution.py:202
  177.9 1.8 place.1
  179.7 22.1 %all_to_all.21.i_ref = bf16[16,32,384]{2,1,0:T(8,128)(2,1)S(1)} all-to-all(bf16[16,32,384]{2,1,0:T(8,128)(2,1)S(1)} %place.1), channel_id=1, replica_groups=mesh['x'=4,'y'=8,'z'=8,'c'=2] {'z','c'}, dimensions={0} | all-to-all | bytes 786432 | tf_op jit(solution)/shard_map/all_to_all | solution.py:202
  201.8 0.9 finish.1
  (39 shorter events, 0.2 us)
Async XLA Ops:
  0.0 1.0 copy-start.7
  1.0 1.0 copy-start.8
  3.2 11.2 %copy-start = (bf16[1024,512]{1,0:T(8,128)(2,1)S(1)}, bf16[1024,512]{1,0:T(8,128)(2,1)}, u32[]{:S(2)}) copy-start(bf16[1024,512]{1,0:T(8,128)(2,1)} %refs_4_.1) | copy-start | bytes 3145732
  3.2 21.1 %copy-start.6 = (bf16[128,1024]{1,0:T(8,128)(2,1)S(1)}, bf16[128,1024]{1,0:T(8,128)(2,1)}, u32[]{:S(2)}) copy-start(bf16[128,1024]{1,0:T(8,128)(2,1)} %mine_ref.1) | copy-start | bytes 786436
  3.2 39.1 %copy-start.17 = (s32[64]{0:T(128)S(1)}, s32[64]{0:T(128)}, u32[]{:S(2)}) copy-start(s32[64]{0:T(128)} %length_ref.1) | copy-start | bytes 772
  3.2 39.1 %copy-start.18 = (s32[2]{0:T(128)S(1)}, s32[2]{0:T(128)}, u32[]{:S(2)}) copy-start(s32[2]{0:T(128)} %cache_ref.1) | copy-start | bytes 28
  3.2 39.1 %all-to-all-start = ((bf16[16,2,128,128]{3,2,1,0:T(8,128)(2,1)}), bf16[16,2,128,128]{3,2,1,0:T(8,128)(2,1)S(1)}, u32[]{:S(2)}, u32[]{:S(2)}) async-start(bf16[16,2,128,128]{3,2,1,0:T(8,128)(2,1)} %bitcast.4), calls=%async_computation | async-start | bytes 2097152 | tf_op jit(solution)/shard_map/all_to_all | solution.py:202
  14.3 53.4 %collective-permute-start.6 = (bf16[1024,512]{1,0:T(8,128)(2,1)S(1)}, bf16[1024,512]{1,0:T(8,128)(2,1)S(1)}, u32[]{:S(2)}, u32[]{:S(2)}) collective-permute-start(bf16[1024,512]{1,0:T(8,128)(2,1)S(1)} %copy-done), channel_id=1, source_target_pairs={{0,128},{128,256},{256,384},{384,0},{1,129},{129,257},{257,385},{3... | collective-permute-start | bytes 3145736 | tf_op jit(solution)/shard_map/ppermute | solution.py:26
  17.5 52.2 %collective-permute-start.8 = (bf16[1024,512]{1,0:T(8,128)(2,1)S(1)}, bf16[1024,512]{1,0:T(8,128)(2,1)}, u32[]{:S(2)}, u32[]{:S(2)}) collective-permute-start(bf16[1024,512]{1,0:T(8,128)(2,1)S(1)} %copy-done), channel_id=1, source_target_pairs={{0,384},{128,0},{256,128},{384,256},{1,385},{129,1},{257,129},{385... | collective-permute-start | bytes 3145736 | tf_op jit(solution)/shard_map/ppermute | solution.py:26
  20.8 51.2 %collective-permute-start.10 = (bf16[1024,512]{1,0:T(8,128)(2,1)S(1)}, bf16[1024,512]{1,0:T(8,128)(2,1)}, u32[]{:S(2)}, u32[]{:S(2)}) collective-permute-start(bf16[1024,512]{1,0:T(8,128)(2,1)S(1)} %copy-done), channel_id=1, source_target_pairs={{0,256},{1,257},{128,384},{129,385},{256,0},{257,1},{384,128},{385... | collective-permute-start | bytes 3145736 | tf_op jit(solution)/shard_map/ppermute | solution.py:31
  25.0 4.0 %collective-permute-start = (bf16[64,1024]{1,0:T(8,128)(2,1)}, bf16[64,1024]{1,0:T(8,128)(2,1)S(1)}, u32[]{:S(2)}, u32[]{:S(2)}) collective-permute-start(bf16[64,1024]{1,0:T(8,128)(2,1)} %constant_dynamic-slice_fusion), channel_id=1, source_target_pairs={{0,1},{1,0},{2,3},{3,2},{4,5},{5,4},{6,7},{7,6},{8,9},{9,8},{10,11... | collective-permute-start | bytes 393224 | tf_op jit(solution)/shard_map/ppermute | solution.py:26
  42.3 1.0 copy-start.9
  43.3 0.9 copy-start.10
  49.3 9.6 %collective-permute-start.1 = (bf16[2,64,1024]{2,1,0:T(8,128)(2,1)S(1)}, bf16[2,64,1024]{2,1,0:T(8,128)(2,1)S(1)}, u32[]{:S(2)}, u32[]{:S(2)}) collective-permute-start(bf16[2,64,1024]{2,1,0:T(8,128)(2,1)S(1)} %attend.1.refs_1_), channel_id=1, source_target_pairs={{0,16},{16,32},{32,48},{48,64},{64,80},{80,96},{96,112},{112,0},{1... | collective-permute-start | bytes 786440 | tf_op jit(solution)/shard_map/ppermute | solution.py:26
  53.7 11.3 %collective-permute-start.2 = (bf16[2,64,1024]{2,1,0:T(8,128)(2,1)S(1)}, bf16[2,64,1024]{2,1,0:T(8,128)(2,1)S(1)}, u32[]{:S(2)}, u32[]{:S(2)}) collective-permute-start(bf16[2,64,1024]{2,1,0:T(8,128)(2,1)S(1)} %attend.1.refs_1_), channel_id=1, source_target_pairs={{0,112},{16,0},{32,16},{48,32},{64,48},{80,64},{96,80},{112,96},{1... | collective-permute-start | bytes 786440 | tf_op jit(solution)/shard_map/ppermute | solution.py:26
  55.7 0.7 copy-start.4
  58.9 15.1 %collective-permute-start.3 = (bf16[2,64,1024]{2,1,0:T(8,128)(2,1)S(1)}, bf16[2,64,1024]{2,1,0:T(8,128)(2,1)S(1)}, u32[]{:S(2)}, u32[]{:S(2)}) collective-permute-start(bf16[2,64,1024]{2,1,0:T(8,128)(2,1)S(1)} %collective-permute-done.1.refs_2_), channel_id=1, source_target_pairs={{0,16},{16,32},{32,48},{48,64},{64,80},{80,96},{96,112},{112,0},{1... | collective-permute-start | bytes 786440 | tf_op jit(solution)/shard_map/ppermute | solution.py:26
  64.3 0.7 copy-start.11
  65.0 11.4 %collective-permute-start.4 = (bf16[2,64,1024]{2,1,0:T(8,128)(2,1)S(1)}, bf16[2,64,1024]{2,1,0:T(8,128)(2,1)}, u32[]{:S(2)}, u32[]{:S(2)}) collective-permute-start(bf16[2,64,1024]{2,1,0:T(8,128)(2,1)S(1)} %collective-permute-done.2.refs_3_), channel_id=1, source_target_pairs={{0,112},{16,0},{32,16},{48,32},{64,48},{80,64},{96,80},{112,96},{1... | collective-permute-start | bytes 786440 | tf_op jit(solution)/shard_map/ppermute | solution.py:26
  67.0 0.7 copy-start.13
  67.7 33.3 %collective-permute-start.5 = (bf16[1024,512]{1,0:T(8,128)(2,1)S(1)}, bf16[1024,512]{1,0:T(8,128)(2,1)S(1)}, u32[]{:S(2)}, u32[]{:S(2)}) collective-permute-start(bf16[1024,512]{1,0:T(8,128)(2,1)S(1)} %copy-done), channel_id=1, source_target_pairs={{0,1},{1,0},{2,3},{3,2},{4,5},{5,4},{6,7},{7,6},{8,9},{9,8},{10,11... | collective-permute-start | bytes 3145736 | tf_op jit(solution)/shard_map/ppermute | solution.py:26
  69.6 31.4 %collective-permute-start.7 = (bf16[1024,512]{1,0:T(8,128)(2,1)S(1)}, bf16[1024,512]{1,0:T(8,128)(2,1)}, u32[]{:S(2)}, u32[]{:S(2)}) collective-permute-start(bf16[1024,512]{1,0:T(8,128)(2,1)S(1)} %collective-permute-done.6.refs_8_.refs_6_), channel_id=1, source_target_pairs={{0,1},{1,0},{2,3},{3,2},{4,5},{5,4},{6,7},{7,6},{8,9},{9,8},{10,11... | collective-permute-start | bytes 3145736 | tf_op jit(solution)/shard_map/ppermute | solution.py:26
  72.0 28.9 %collective-permute-start.9 = (bf16[1024,512]{1,0:T(8,128)(2,1)}, bf16[1024,512]{1,0:T(8,128)(2,1)}, u32[]{:S(2)}, u32[]{:S(2)}) collective-permute-start(bf16[1024,512]{1,0:T(8,128)(2,1)} %collective-permute-done.8.refs_10_.refs_8_), channel_id=1, source_target_pairs={{0,1},{1,0},{2,3},{3,2},{4,5},{5,4},{6,7},{7,6},{8,9},{9,8},{10,11... | collective-permute-start | bytes 3145736 | tf_op jit(solution)/shard_map/ppermute | solution.py:26
  74.0 27.0 %collective-permute-start.11 = (bf16[1024,512]{1,0:T(8,128)(2,1)}, bf16[1024,512]{1,0:T(8,128)(2,1)}, u32[]{:S(2)}, u32[]{:S(2)}) collective-permute-start(bf16[1024,512]{1,0:T(8,128)(2,1)} %collective-permute-done.10.refs_12_.refs_10_), channel_id=1, source_target_pairs={{0,1},{1,0},{2,3},{3,2},{4,5},{5,4},{6,7},{7,6},{8,9},{9,8},{10,11... | collective-permute-start | bytes 3145736 | tf_op jit(solution)/shard_map/ppermute | solution.py:26
  76.5 10.1 %collective-permute-start.12 = (bf16[2,64,1024]{2,1,0:T(8,128)(2,1)S(1)}, bf16[2,64,1024]{2,1,0:T(8,128)(2,1)S(1)}, u32[]{:S(2)}, u32[]{:S(2)}) collective-permute-start(bf16[2,64,1024]{2,1,0:T(8,128)(2,1)S(1)} %collective-permute-done.3.refs_4_), channel_id=1, source_target_pairs={{0,16},{16,32},{32,48},{48,64},{64,80},{80,96},{96,112},{112,0},{1... | collective-permute-start | bytes 786440 | tf_op jit(solution)/shard_map/ppermute | solution.py:26
  81.0 0.7 copy-start.15
  86.6 11.4 %collective-permute-start.13 = (bf16[2,64,1024]{2,1,0:T(8,128)(2,1)}, bf16[2,64,1024]{2,1,0:T(8,128)(2,1)}, u32[]{:S(2)}, u32[]{:S(2)}) collective-permute-start(bf16[2,64,1024]{2,1,0:T(8,128)(2,1)} %collective-permute-done.4.refs_5_), channel_id=1, source_target_pairs={{0,112},{16,0},{32,16},{48,32},{64,48},{80,64},{96,80},{112,96},{1... | collective-permute-start | bytes 786440 | tf_op jit(solution)/shard_map/ppermute | solution.py:26
  99.0 8.3 %collective-permute-start.14 = (bf16[2,64,1024]{2,1,0:T(8,128)(2,1)S(1)}, bf16[2,64,1024]{2,1,0:T(8,128)(2,1)S(1)}, u32[]{:S(2)}, u32[]{:S(2)}) collective-permute-start(bf16[2,64,1024]{2,1,0:T(8,128)(2,1)S(1)} %broadcast_select_fusion), channel_id=1, source_target_pairs={{0,16},{1,113},{16,32},{17,1},{32,48},{33,17},{48,64},{49,33},{64,... | collective-permute-start | bytes 786440 | tf_op jit(solution)/shard_map/ppermute | solution.py:31
  101.0 11.0 %copy-start.1 = (bf16[1024,512]{1,0:T(8,128)(2,1)}, bf16[1024,512]{1,0:T(8,128)(2,1)S(1)}, u32[]{:S(2)}) copy-start(bf16[1024,512]{1,0:T(8,128)(2,1)S(1)} %collective-permute-done.5.refs_7_.refs_5_) | copy-start | bytes 3145732
  111.9 0.9 copy-start.3
  112.9 25.8 %all-to-all-start.2 = ((bf16[32,32,384]{2,1,0:T(8,128)(2,1)}), bf16[32,32,384]{2,1,0:T(8,128)(2,1)}, u32[]{:S(2)}, u32[]{:S(2)}) async-start(bf16[32,32,384]{2,1,0:T(8,128)(2,1)} %bitcast.11), calls=%async_computation.2 | async-start | bytes 1572864 | tf_op jit(solution)/shard_map/all_to_all | solution.py:202
  119.1 1.2 copy-start.2
  120.3 0.9 copy-start.5
  121.2 0.9 copy-start.12
  122.2 0.9 copy-start.14
  123.1 0.9 copy-start.16
  138.7 39.2 %copy-start.19 = (s32[64]{0:T(128)S(1)}, s32[64]{0:T(128)}, u32[]{:S(2)}) copy-start(s32[64]{0:T(128)} %group_ref.1) | copy-start | bytes 772
  138.7 39.2 %copy-start.20 = (s32[64]{0:T(128)S(1)}, s32[64]{0:T(128)}, u32[]{:S(2)}) copy-start(s32[64]{0:T(128)} %first_ref.1) | copy-start | bytes 772
where the time goes:
time: 204 us; the launch traced here: 203 us
  blocking collectives  61.3 us (30%)
  starting transfers between devices  60.7 us (30%)
  waiting for transfers between devices  46.8 us (23%)
  Pallas kernels  19 us (9%)
  local copies, waits for them, and re-layouts  13.4 us (7%)
    all_to_all x2, blocking collectives, exchange(): return lax.all_to_all(value, axes, 0, 0, tiled=True)  61.3 us
    ppermute x13, starting transfers between devices, shift(): lax.ppermute(value, axis, [(i, (i + step) % size) for i in range(size)])  38 us
    all_to_all x2, waiting for transfers between devices, exchange(): return lax.all_to_all(value, axes, 0, 0, tiled=True)  22.3 us
    ppermute x13, waiting for transfers between devices, shift(): lax.ppermute(value, axis, [(i, (i + step) % size) for i in range(size)])  18.2 us
    all_to_all x2, starting transfers between devices, exchange(): return lax.all_to_all(value, axes, 0, 0, tiled=True)  17.3 us
    unnamed x42, local copies, waits for them, and re-layouts  12.7 us
    pallas_call x2, Pallas kernels, project(): pl.pallas_call(lambda *refs: project_kernel(count, *refs), in_specs=[SMEM...  10.2 us
    ppermute x2, waiting for transfers between devices, shift_cores(): return lax.ppermute(value, (axis, 'c'), pairs)  6.35 us
  transfers between devices with their start and end apart: 17, of which 8 were waited for; matrix products, arithmetic and copies ran while one was open for 1% of the time, Pallas kernels for 5%

commit v1 on v0

--- a/solution.py
+++ b/solution.py
@@ -35,6 +35,10 @@
     return pltpu.with_memory_space_constraint(value, pltpu.VMEM)
 
 
+def far_off(value):
+    return pltpu.with_memory_space_constraint(value, pltpu.HBM)
+
+
 def kv_kernel(k_ref, v_ref, o_ref):
     for h in range(NZ):
         o_ref[h, 0, 0] = k_ref[0, :, h * HEAD_DIM : (h + 1) * HEAD_DIM]
@@ -50,7 +54,7 @@
         out_shape=pltpu.VMEM((NZ, 2, 2, 128, 128), BF16),
         compiler_params=PARAMS,
         name="pack_kv",
-    )(k, v)
+    )(far_off(k), far_off(v))
 
 
 def attend_kernel(s_ref, cache_ref, draft_ref, mine_ref, other_ref, kv_ref, dk_ref, dv_ref, o_ref):
@@ -103,7 +107,7 @@
         out_shape=pltpu.VMEM((2, DRAFT, 1024), BF16),
         compiler_params=PARAMS,
         name="attend",
-    )(ids, cache_lengths, draft_lengths, q, other_q, kv, dk, dv)
+    )(ids, cache_lengths, draft_lengths, far_off(q), other_q, kv, far_off(dk), far_off(dv))
 
 
 def project_kernel(count, s_ref, *refs):
@@ -229,9 +233,9 @@
 
     rows = attend(ids, cache_lengths, draft_lengths, queries, other_q, kv, draft_keys, draft_values)
     up1, down1 = shift(rows, "y", NY, 1), shift(rows, "y", NY, -1)
-    up2, down2 = shift(up1, "y", NY, 1), shift(down1, "y", NY, -1)
+    up2, down2 = shift(rows, "y", NY, 2), shift(rows, "y", NY, -2)
     up3, down3 = shift(up2, "y", NY, 1), shift(down2, "y", NY, -1)
-    far = shift_cores(jnp.where(c == 0, up3, down3), "y", NY, 1)
+    far = shift_cores(jnp.where(c == 0, up2, down2), "y", NY, 2)
     arrived = {0: rows, -1: up1, 1: down1, -2: up2, 2: down2, -3: up3, 3: down3, -4: far}
 
     sums = []

time: 204 us -> 235 us (1.15)
  the two profiles are of different devices: /device:TPU:25 before, /device:TPU:1 now
where the time goes in v1:
time: 235 us; the launch traced here: 234 us
  starting transfers between devices  95.1 us (40%)
  blocking collectives  62.7 us (27%)
  waiting for transfers between devices  49.8 us (21%)
  Pallas kernels  22.2 us (9%)
  local copies, waits for them, and re-layouts  3.56 us (2%)
    ppermute x13, starting transfers between devices, shift(): lax.ppermute(value, axis, [(i, (i + step) % size) for i in range(size)])  64.3 us
    all_to_all x2, blocking collectives, exchange(): return lax.all_to_all(value, axes, 0, 0, tiled=True)  62.7 us
    ppermute x13, waiting for transfers between devices, shift(): lax.ppermute(value, axis, [(i, (i + step) % size) for i in range(size)])  41.7 us
    all_to_all x2, starting transfers between devices, exchange(): return lax.all_to_all(value, axes, 0, 0, tiled=True)  22.2 us
    pallas_call x2, Pallas kernels, project(): pl.pallas_call(lambda *refs: project_kernel(count, *refs), in_specs=[SMEM...  11.6 us
    ppermute x2, starting transfers between devices, shift_cores(): return lax.ppermute(value, (axis, 'c'), pairs)  8.55 us
    ppermute x2, waiting for transfers between devices, shift_cores(): return lax.ppermute(value, (axis, 'c'), pairs)  8.13 us
    pallas_call x1, Pallas kernels, attend(): pl.pallas_call(attend_kernel, grid_spec=pltpu.PrefetchScalarGridSpec(num_...  5.87 us
  transfers between devices with their start and end apart: 17, of which 7 were waited for; matrix products, arithmetic and copies ran while one was open for 0% of the time, Pallas kernels for 5%

profile of v1, /device:TPU:1, one launch (start us, length us, event | category | flops | bytes accessed | tf_op | source)
XLA Modules:
  0.0 233.7 jit_solution(5754645733531397593)
XLA Ops:
  0.0 2.1 pack_kv.1
  2.1 0.0 copy-start.8
  2.1 12.0 %all-to-all-start = ((bf16[16,2,128,128]{3,2,1,0:T(8,128)(2,1)}), bf16[16,2,128,128]{3,2,1,0:T(8,128)(2,1)S(1)}, u32[]{:S(2)}, u32[]{:S(2)}) async-start(bf16[16,2,128,128]{3,2,1,0:T(8,128)(2,1)} %bitcast.4), calls=%async_computation | async-start | bytes 2097152 | tf_op jit(solution)/shard_map/all_to_all | solution.py:206
  14.1 3.1 %collective-permute-start.6 = (bf16[1024,512]{1,0:T(8,128)(2,1)S(1)}, bf16[1024,512]{1,0:T(8,128)(2,1)S(1)}, u32[]{:S(2)}, u32[]{:S(2)}) collective-permute-start(bf16[1024,512]{1,0:T(8,128)(2,1)S(1)} %copy-done), channel_id=1, source_target_pairs={{0,128},{128,256},{256,384},{384,0},{1,129},{129,257},{257,385},{3... | collective-permute-start | bytes 3145736 | tf_op jit(solution)/shard_map/ppermute | solution.py:26
  17.2 3.4 %collective-permute-start.8 = (bf16[1024,512]{1,0:T(8,128)(2,1)S(1)}, bf16[1024,512]{1,0:T(8,128)(2,1)}, u32[]{:S(2)}, u32[]{:S(2)}) collective-permute-start(bf16[1024,512]{1,0:T(8,128)(2,1)S(1)} %copy-done), channel_id=1, source_target_pairs={{0,384},{128,0},{256,128},{384,256},{1,385},{129,1},{257,129},{385... | collective-permute-start | bytes 3145736 | tf_op jit(solution)/shard_map/ppermute | solution.py:26
  20.6 3.4 %collective-permute-start.10 = (bf16[1024,512]{1,0:T(8,128)(2,1)S(1)}, bf16[1024,512]{1,0:T(8,128)(2,1)}, u32[]{:S(2)}, u32[]{:S(2)}) collective-permute-start(bf16[1024,512]{1,0:T(8,128)(2,1)S(1)} %copy-done), channel_id=1, source_target_pairs={{0,256},{1,257},{128,384},{129,385},{256,0},{257,1},{384,128},{385... | collective-permute-start | bytes 3145736 | tf_op jit(solution)/shard_map/ppermute | solution.py:31
  24.0 2.9 %collective-permute-start.5 = (bf16[1024,512]{1,0:T(8,128)(2,1)S(1)}, bf16[1024,512]{1,0:T(8,128)(2,1)}, u32[]{:S(2)}, u32[]{:S(2)}) collective-permute-start(bf16[1024,512]{1,0:T(8,128)(2,1)S(1)} %copy-done), channel_id=1, source_target_pairs={{0,1},{1,0},{2,3},{3,2},{4,5},{5,4},{6,7},{7,6},{8,9},{9,8},{10,11... | collective-permute-start | bytes 3145736 | tf_op jit(solution)/shard_map/ppermute | solution.py:26
  26.9 14.9 %collective-permute-done.6.refs_8_.refs_6_ = bf16[1024,512]{1,0:T(8,128)(2,1)S(1)} collective-permute-done((bf16[1024,512]{1,0:T(8,128)(2,1)S(1)}, bf16[1024,512]{1,0:T(8,128)(2,1)S(1)}, u32[]{:S(2)}, u32[]{:S(2)}) %collective-permute-start.6) | collective-permute-done | bytes 1048608 | tf_op jit(solution)/shard_map/ppermute | solution.py:26
  41.8 2.9 %collective-permute-start.7 = (bf16[1024,512]{1,0:T(8,128)(2,1)S(1)}, bf16[1024,512]{1,0:T(8,128)(2,1)}, u32[]{:S(2)}, u32[]{:S(2)}) collective-permute-start(bf16[1024,512]{1,0:T(8,128)(2,1)S(1)} %collective-permute-done.6.refs_8_.refs_6_), channel_id=1, source_target_pairs={{0,1},{1,0},{2,3},{3,2},{4,5},{5,4},{6,7},{7,6},{8,9},{9,8},{10,11... | collective-permute-start | bytes 3145736 | tf_op jit(solution)/shard_map/ppermute | solution.py:26
  44.7 0.7 constant_dynamic-slice_fusion
  45.4 1.9 collective-permute-start
  47.3 0.0 collective-permute-done.8.refs_10_.refs_8_
  47.3 21.1 %collective-permute-start.9 = (bf16[1024,512]{1,0:T(8,128)(2,1)}, bf16[1024,512]{1,0:T(8,128)(2,1)}, u32[]{:S(2)}, u32[]{:S(2)}) collective-permute-start(bf16[1024,512]{1,0:T(8,128)(2,1)} %collective-permute-done.8.refs_10_.refs_8_), channel_id=1, source_target_pairs={{0,1},{1,0},{2,3},{3,2},{4,5},{5,4},{6,7},{7,6},{8,9},{9,8},{10,11... | collective-permute-start | bytes 3145736 | tf_op jit(solution)/shard_map/ppermute | solution.py:26
  68.4 0.0 collective-permute-done.10.refs_12_.refs_10_
  68.4 1.9 collective-permute-start.11
  70.3 0.1 pad_add_fusion.s_ref.refs_0_
  70.4 0.0 collective-permute-done.other_ref
  70.4 0.0 all-to-all-done.kv_ref
  70.4 5.9 %attend.1.refs_1_ = bf16[2,64,1024]{2,1,0:T(8,128)(2,1)S(1)} custom-call(s32[4]{0:T(128)S(1)} %pad_add_fusion.s_ref.refs_0_, s32[2]{0:T(128)S(1)} %copy-done.8, s32[64]{0:T(128)S(1)} %copy-done.7, bf16[128,1024]{1,0:T(8,128)(2,1)} %mine_ref.1, bf16[64,1024]{1,0:T(8,128)(2,1)S(1)} %collective-permute-done.other_ref, ...), custom_call_target="tpu_custom_call" | custom-call | tf_op jit(solution)/shard_map/attend/pallas_call | solution.py:93
  76.3 4.2 %collective-permute-start.3 = (bf16[2,64,1024]{2,1,0:T(8,128)(2,1)S(1)}, bf16[2,64,1024]{2,1,0:T(8,128)(2,1)S(1)}, u32[]{:S(2)}, u32[]{:S(2)}) collective-permute-start(bf16[2,64,1024]{2,1,0:T(8,128)(2,1)S(1)} %attend.1.refs_1_), channel_id=1, source_target_pairs={{0,32},{16,48},{32,64},{48,80},{64,96},{80,112},{96,0},{112,16},{1... | collective-permute-start | bytes 786440 | tf_op jit(solution)/shard_map/ppermute | solution.py:26
  80.5 10.8 %collective-permute-done.3.refs_4_ = bf16[2,64,1024]{2,1,0:T(8,128)(2,1)S(1)} collective-permute-done((bf16[2,64,1024]{2,1,0:T(8,128)(2,1)S(1)}, bf16[2,64,1024]{2,1,0:T(8,128)(2,1)S(1)}, u32[]{:S(2)}, u32[]{:S(2)}) %collective-permute-start.3) | collective-permute-done | bytes 262176 | tf_op jit(solution)/shard_map/ppermute | solution.py:26
  91.3 3.1 %collective-permute-start.4 = (bf16[2,64,1024]{2,1,0:T(8,128)(2,1)S(1)}, bf16[2,64,1024]{2,1,0:T(8,128)(2,1)S(1)}, u32[]{:S(2)}, u32[]{:S(2)}) collective-permute-start(bf16[2,64,1024]{2,1,0:T(8,128)(2,1)S(1)} %attend.1.refs_1_), channel_id=1, source_target_pairs={{0,96},{16,112},{32,0},{48,16},{64,32},{80,48},{96,64},{112,80},{1... | collective-permute-start | bytes 786440 | tf_op jit(solution)/shard_map/ppermute | solution.py:26
  94.4 5.5 %collective-permute-done.4.refs_5_ = bf16[2,64,1024]{2,1,0:T(8,128)(2,1)S(1)} collective-permute-done((bf16[2,64,1024]{2,1,0:T(8,128)(2,1)S(1)}, bf16[2,64,1024]{2,1,0:T(8,128)(2,1)S(1)}, u32[]{:S(2)}, u32[]{:S(2)}) %collective-permute-start.4) | collective-permute-done | bytes 262176 | tf_op jit(solution)/shard_map/ppermute | solution.py:26
  99.9 9.2 %collective-permute-start.12 = (bf16[2,64,1024]{2,1,0:T(8,128)(2,1)S(1)}, bf16[2,64,1024]{2,1,0:T(8,128)(2,1)S(1)}, u32[]{:S(2)}, u32[]{:S(2)}) collective-permute-start(bf16[2,64,1024]{2,1,0:T(8,128)(2,1)S(1)} %collective-permute-done.3.refs_4_), channel_id=1, source_target_pairs={{0,16},{16,32},{32,48},{48,64},{64,80},{80,96},{96,112},{112,0},{1... | collective-permute-start | bytes 786440 | tf_op jit(solution)/shard_map/ppermute | solution.py:26
  109.2 0.0 collective-permute-done.5.refs_7_.refs_5_
  109.2 4.2 %collective-permute-start.13 = (bf16[2,64,1024]{2,1,0:T(8,128)(2,1)S(1)}, bf16[2,64,1024]{2,1,0:T(8,128)(2,1)S(1)}, u32[]{:S(2)}, u32[]{:S(2)}) collective-permute-start(bf16[2,64,1024]{2,1,0:T(8,128)(2,1)S(1)} %collective-permute-done.4.refs_5_), channel_id=1, source_target_pairs={{0,112},{16,0},{32,16},{48,32},{64,48},{80,64},{96,80},{112,96},{1... | collective-permute-start | bytes 786440 | tf_op jit(solution)/shard_map/ppermute | solution.py:26
  113.4 0.0 collective-permute-done.7.refs_9_.refs_7_
  113.4 5.1 %collective-permute-start.14 = (bf16[2,64,1024]{2,1,0:T(8,128)(2,1)S(1)}, bf16[2,64,1024]{2,1,0:T(8,128)(2,1)S(1)}, u32[]{:S(2)}, u32[]{:S(2)}) collective-permute-start(bf16[2,64,1024]{2,1,0:T(8,128)(2,1)S(1)} %broadcast_select_fusion), channel_id=1, source_target_pairs={{0,32},{1,97},{16,48},{17,113},{32,64},{33,1},{48,80},{49,17},{64,... | collective-permute-start | bytes 786440 | tf_op jit(solution)/shard_map/ppermute | solution.py:31
  118.5 0.0 collective-permute-done.9.refs_11_.refs_9_
  118.5 3.5 %collective-permute-done.13.refs_2_ = bf16[2,64,1024]{2,1,0:T(8,128)(2,1)S(1)} collective-permute-done((bf16[2,64,1024]{2,1,0:T(8,128)(2,1)S(1)}, bf16[2,64,1024]{2,1,0:T(8,128)(2,1)S(1)}, u32[]{:S(2)}, u32[]{:S(2)}) %collective-permute-start.13) | collective-permute-done | bytes 262176 | tf_op jit(solution)/shard_map/ppermute | solution.py:26
  122.1 8.1 %collective-permute-done.14.refs_3_ = bf16[2,64,1024]{2,1,0:T(8,128)(2,1)S(1)} collective-permute-done((bf16[2,64,1024]{2,1,0:T(8,128)(2,1)S(1)}, bf16[2,64,1024]{2,1,0:T(8,128)(2,1)S(1)}, u32[]{:S(2)}, u32[]{:S(2)}) %collective-permute-start.14) | collective-permute-done | bytes 262176 | tf_op jit(solution)/shard_map/ppermute | solution.py:31
  130.2 5.7 %project.3 = bf16[4,8,32,384]{3,2,1,0:T(8,128)(2,1)} custom-call(s32[4]{0:T(128)S(1)} %pad_add_fusion.s_ref.refs_0_, bf16[2,64,1024]{2,1,0:T(8,128)(2,1)S(1)} %collective-permute-done.12.refs_1_, bf16[2,64,1024]{2,1,0:T(8,128)(2,1)S(1)} %collective-permute-done.13.refs_2_, bf16[2,64,1024]{2,1,0:T(8,128)(2,1)S(1)} %collective-permute-done.14.refs_3_, ...), custom_call_target="tpu_custom_call" | custom-call | tf_op jit(solution)/shard_map/project/pallas_call | solution.py:129
  135.9 10.3 %all-to-all-start.2 = ((bf16[32,32,384]{2,1,0:T(8,128)(2,1)}), bf16[32,32,384]{2,1,0:T(8,128)(2,1)}, u32[]{:S(2)}, u32[]{:S(2)}) async-start(bf16[32,32,384]{2,1,0:T(8,128)(2,1)} %bitcast.7), calls=%async_computation.2 | async-start | bytes 1572864 | tf_op jit(solution)/shard_map/all_to_all | solution.py:206
  146.2 1.9 collective-permute-start.1
  148.1 4.6 %collective-permute-start.2 = (bf16[2,64,1024]{2,1,0:T(8,128)(2,1)S(1)}, bf16[2,64,1024]{2,1,0:T(8,128)(2,1)S(1)}, u32[]{:S(2)}, u32[]{:S(2)}) collective-permute-start(bf16[2,64,1024]{2,1,0:T(8,128)(2,1)S(1)} %attend.1.refs_1_), channel_id=1, source_target_pairs={{0,112},{16,0},{32,16},{48,32},{64,48},{80,64},{96,80},{112,96},{1... | collective-permute-start | bytes 786440 | tf_op jit(solution)/shard_map/ppermute | solution.py:26
  152.7 4.0 %collective-permute-done.1.refs_2_ = bf16[2,64,1024]{2,1,0:T(8,128)(2,1)S(1)} collective-permute-done((bf16[2,64,1024]{2,1,0:T(8,128)(2,1)S(1)}, bf16[2,64,1024]{2,1,0:T(8,128)(2,1)S(1)}, u32[]{:S(2)}, u32[]{:S(2)}) %collective-permute-start.1) | collective-permute-done | bytes 262176 | tf_op jit(solution)/shard_map/ppermute | solution.py:26
  156.7 2.9 %collective-permute-done.2.refs_3_ = bf16[2,64,1024]{2,1,0:T(8,128)(2,1)S(1)} collective-permute-done((bf16[2,64,1024]{2,1,0:T(8,128)(2,1)S(1)}, bf16[2,64,1024]{2,1,0:T(8,128)(2,1)S(1)}, u32[]{:S(2)}, u32[]{:S(2)}) %collective-permute-start.2) | collective-permute-done | bytes 262176 | tf_op jit(solution)/shard_map/ppermute | solution.py:26
  159.6 0.9 copy-done.2
  160.6 0.9 copy-done.4
  161.5 0.9 copy-done.6
  162.5 5.9 %project.2 = bf16[4,8,32,640]{3,2,1,0:T(8,128)(2,1)S(1)} custom-call(s32[4]{0:T(128)S(1)} %pad_add_fusion.s_ref.refs_0_, bf16[2,64,1024]{2,1,0:T(8,128)(2,1)S(1)} %copy-done.2, bf16[2,64,1024]{2,1,0:T(8,128)(2,1)S(1)} %collective-permute-done.1.refs_2_, bf16[2,64,1024]{2,1,0:T(8,128)(2,1)S(1)} %collective-permute-done.2.refs_3_, ...), custom_call_target="tpu_custom_call" | custom-call | tf_op jit(solution)/shard_map/project/pallas_call | solution.py:129
  168.4 0.0 all-to-all-done.2
  168.4 0.0 copy-start.9
  168.4 0.0 copy-start.10
  168.4 42.7 %all_to_all.20 = bf16[32,32,640]{2,1,0:T(8,128)(2,1)S(1)} all-to-all(bf16[32,32,640]{2,1,0:T(8,128)(2,1)S(1)} %bitcast.10), channel_id=1, replica_groups=mesh['x'=4,'y'=8,'z'=8,'c'=2] {'x','z'}, dimensions={0} | all-to-all | bytes 2621440 | tf_op jit(solution)/shard_map/all_to_all | solution.py:206
  211.1 1.8 place.1
  212.9 20.0 %all_to_all.21.i_ref = bf16[16,32,384]{2,1,0:T(8,128)(2,1)S(1)} all-to-all(bf16[16,32,384]{2,1,0:T(8,128)(2,1)S(1)} %place.1), channel_id=1, replica_groups=mesh['x'=4,'y'=8,'z'=8,'c'=2] {'z','c'}, dimensions={0} | all-to-all | bytes 786432 | tf_op jit(solution)/shard_map/all_to_all | solution.py:206
  232.9 0.9 finish.1
  (21 shorter events, 0.1 us)
Async XLA Ops:
  2.1 12.0 %copy-start = (bf16[1024,512]{1,0:T(8,128)(2,1)S(1)}, bf16[1024,512]{1,0:T(8,128)(2,1)}, u32[]{:S(2)}) copy-start(bf16[1024,512]{1,0:T(8,128)(2,1)} %refs_4_.1) | copy-start | bytes 3145732
  2.1 42.6 %copy-start.11 = (bf16[128,1024]{1,0:T(8,128)(2,1)S(1)}, bf16[128,1024]{1,0:T(8,128)(2,1)}, u32[]{:S(2)}) copy-start(bf16[128,1024]{1,0:T(8,128)(2,1)} %mine_ref.1) | copy-start | bytes 786436
  2.1 68.3 %copy-start.7 = (s32[64]{0:T(128)S(1)}, s32[64]{0:T(128)}, u32[]{:S(2)}) copy-start(s32[64]{0:T(128)} %length_ref.1) | copy-start | bytes 772
  2.1 68.3 %copy-start.8 = (s32[2]{0:T(128)S(1)}, s32[2]{0:T(128)}, u32[]{:S(2)}) copy-start(s32[2]{0:T(128)} %cache_ref.1) | copy-start | bytes 28
  2.1 68.3 %all-to-all-start = ((bf16[16,2,128,128]{3,2,1,0:T(8,128)(2,1)}), bf16[16,2,128,128]{3,2,1,0:T(8,128)(2,1)S(1)}, u32[]{:S(2)}, u32[]{:S(2)}) async-start(bf16[16,2,128,128]{3,2,1,0:T(8,128)(2,1)} %bitcast.4), calls=%async_computation | async-start | bytes 2097152 | tf_op jit(solution)/shard_map/all_to_all | solution.py:206
  14.1 27.7 %collective-permute-start.6 = (bf16[1024,512]{1,0:T(8,128)(2,1)S(1)}, bf16[1024,512]{1,0:T(8,128)(2,1)S(1)}, u32[]{:S(2)}, u32[]{:S(2)}) collective-permute-start(bf16[1024,512]{1,0:T(8,128)(2,1)S(1)} %copy-done), channel_id=1, source_target_pairs={{0,128},{128,256},{256,384},{384,0},{1,129},{129,257},{257,385},{3... | collective-permute-start | bytes 3145736 | tf_op jit(solution)/shard_map/ppermute | solution.py:26
  17.2 30.1 %collective-permute-start.8 = (bf16[1024,512]{1,0:T(8,128)(2,1)S(1)}, bf16[1024,512]{1,0:T(8,128)(2,1)}, u32[]{:S(2)}, u32[]{:S(2)}) collective-permute-start(bf16[1024,512]{1,0:T(8,128)(2,1)S(1)} %copy-done), channel_id=1, source_target_pairs={{0,384},{128,0},{256,128},{384,256},{1,385},{129,1},{257,129},{385... | collective-permute-start | bytes 3145736 | tf_op jit(solution)/shard_map/ppermute | solution.py:26
  20.6 47.8 %collective-permute-start.10 = (bf16[1024,512]{1,0:T(8,128)(2,1)S(1)}, bf16[1024,512]{1,0:T(8,128)(2,1)}, u32[]{:S(2)}, u32[]{:S(2)}) collective-permute-start(bf16[1024,512]{1,0:T(8,128)(2,1)S(1)} %copy-done), channel_id=1, source_target_pairs={{0,256},{1,257},{128,384},{129,385},{256,0},{257,1},{384,128},{385... | collective-permute-start | bytes 3145736 | tf_op jit(solution)/shard_map/ppermute | solution.py:31
  24.0 85.2 %collective-permute-start.5 = (bf16[1024,512]{1,0:T(8,128)(2,1)S(1)}, bf16[1024,512]{1,0:T(8,128)(2,1)}, u32[]{:S(2)}, u32[]{:S(2)}) collective-permute-start(bf16[1024,512]{1,0:T(8,128)(2,1)S(1)} %copy-done), channel_id=1, source_target_pairs={{0,1},{1,0},{2,3},{3,2},{4,5},{5,4},{6,7},{7,6},{8,9},{9,8},{10,11... | collective-permute-start | bytes 3145736 | tf_op jit(solution)/shard_map/ppermute | solution.py:26
  41.8 71.6 %collective-permute-start.7 = (bf16[1024,512]{1,0:T(8,128)(2,1)S(1)}, bf16[1024,512]{1,0:T(8,128)(2,1)}, u32[]{:S(2)}, u32[]{:S(2)}) collective-permute-start(bf16[1024,512]{1,0:T(8,128)(2,1)S(1)} %collective-permute-done.6.refs_8_.refs_6_), channel_id=1, source_target_pairs={{0,1},{1,0},{2,3},{3,2},{4,5},{5,4},{6,7},{7,6},{8,9},{9,8},{10,11... | collective-permute-start | bytes 3145736 | tf_op jit(solution)/shard_map/ppermute | solution.py:26
  45.4 25.0 %collective-permute-start = (bf16[64,1024]{1,0:T(8,128)(2,1)}, bf16[64,1024]{1,0:T(8,128)(2,1)S(1)}, u32[]{:S(2)}, u32[]{:S(2)}) collective-permute-start(bf16[64,1024]{1,0:T(8,128)(2,1)} %constant_dynamic-slice_fusion), channel_id=1, source_target_pairs={{0,1},{1,0},{2,3},{3,2},{4,5},{5,4},{6,7},{7,6},{8,9},{9,8},{10,11... | collective-permute-start | bytes 393224 | tf_op jit(solution)/shard_map/ppermute | solution.py:26
  47.3 71.2 %collective-permute-start.9 = (bf16[1024,512]{1,0:T(8,128)(2,1)}, bf16[1024,512]{1,0:T(8,128)(2,1)}, u32[]{:S(2)}, u32[]{:S(2)}) collective-permute-start(bf16[1024,512]{1,0:T(8,128)(2,1)} %collective-permute-done.8.refs_10_.refs_8_), channel_id=1, source_target_pairs={{0,1},{1,0},{2,3},{3,2},{4,5},{5,4},{6,7},{7,6},{8,9},{9,8},{10,11... | collective-permute-start | bytes 3145736 | tf_op jit(solution)/shard_map/ppermute | solution.py:26
  68.4 50.2 %collective-permute-start.11 = (bf16[1024,512]{1,0:T(8,128)(2,1)}, bf16[1024,512]{1,0:T(8,128)(2,1)}, u32[]{:S(2)}, u32[]{:S(2)}) collective-permute-start(bf16[1024,512]{1,0:T(8,128)(2,1)} %collective-permute-done.10.refs_12_.refs_10_), channel_id=1, source_target_pairs={{0,1},{1,0},{2,3},{3,2},{4,5},{5,4},{6,7},{7,6},{8,9},{9,8},{10,11... | collective-permute-start | bytes 3145736 | tf_op jit(solution)/shard_map/ppermute | solution.py:26
  76.3 71.8 %copy-start.1 = (bf16[2,64,1024]{2,1,0:T(8,128)(2,1)}, bf16[2,64,1024]{2,1,0:T(8,128)(2,1)S(1)}, u32[]{:S(2)}) copy-start(bf16[2,64,1024]{2,1,0:T(8,128)(2,1)S(1)} %attend.1.refs_1_) | copy-start | bytes 786436
  76.3 15.0 %collective-permute-start.3 = (bf16[2,64,1024]{2,1,0:T(8,128)(2,1)S(1)}, bf16[2,64,1024]{2,1,0:T(8,128)(2,1)S(1)}, u32[]{:S(2)}, u32[]{:S(2)}) collective-permute-start(bf16[2,64,1024]{2,1,0:T(8,128)(2,1)S(1)} %attend.1.refs_1_), channel_id=1, source_target_pairs={{0,32},{16,48},{32,64},{48,80},{64,96},{80,112},{96,0},{112,16},{1... | collective-permute-start | bytes 786440 | tf_op jit(solution)/shard_map/ppermute | solution.py:26
  91.3 44.6 %copy-start.3 = (bf16[2,64,1024]{2,1,0:T(8,128)(2,1)}, bf16[2,64,1024]{2,1,0:T(8,128)(2,1)S(1)}, u32[]{:S(2)}) copy-start(bf16[2,64,1024]{2,1,0:T(8,128)(2,1)S(1)} %collective-permute-done.3.refs_4_) | copy-start | bytes 786436
  91.3 8.6 %collective-permute-start.4 = (bf16[2,64,1024]{2,1,0:T(8,128)(2,1)S(1)}, bf16[2,64,1024]{2,1,0:T(8,128)(2,1)S(1)}, u32[]{:S(2)}, u32[]{:S(2)}) collective-permute-start(bf16[2,64,1024]{2,1,0:T(8,128)(2,1)S(1)} %attend.1.refs_1_), channel_id=1, source_target_pairs={{0,96},{16,112},{32,0},{48,16},{64,32},{80,48},{96,64},{112,80},{1... | collective-permute-start | bytes 786440 | tf_op jit(solution)/shard_map/ppermute | solution.py:26
  99.9 36.0 %copy-start.5 = (bf16[2,64,1024]{2,1,0:T(8,128)(2,1)}, bf16[2,64,1024]{2,1,0:T(8,128)(2,1)S(1)}, u32[]{:S(2)}) copy-start(bf16[2,64,1024]{2,1,0:T(8,128)(2,1)S(1)} %collective-permute-done.4.refs_5_) | copy-start | bytes 786436
  99.9 18.6 %collective-permute-start.12 = (bf16[2,64,1024]{2,1,0:T(8,128)(2,1)S(1)}, bf16[2,64,1024]{2,1,0:T(8,128)(2,1)S(1)}, u32[]{:S(2)}, u32[]{:S(2)}) collective-permute-start(bf16[2,64,1024]{2,1,0:T(8,128)(2,1)S(1)} %collective-permute-done.3.refs_4_), channel_id=1, source_target_pairs={{0,16},{16,32},{32,48},{48,64},{64,80},{80,96},{96,112},{112,0},{1... | collective-permute-start | bytes 786440 | tf_op jit(solution)/shard_map/ppermute | solution.py:26
  109.2 12.9 %collective-permute-start.13 = (bf16[2,64,1024]{2,1,0:T(8,128)(2,1)S(1)}, bf16[2,64,1024]{2,1,0:T(8,128)(2,1)S(1)}, u32[]{:S(2)}, u32[]{:S(2)}) collective-permute-start(bf16[2,64,1024]{2,1,0:T(8,128)(2,1)S(1)} %collective-permute-done.4.refs_5_), channel_id=1, source_target_pairs={{0,112},{16,0},{32,16},{48,32},{64,48},{80,64},{96,80},{112,96},{1... | collective-permute-start | bytes 786440 | tf_op jit(solution)/shard_map/ppermute | solution.py:26
  113.4 16.8 %collective-permute-start.14 = (bf16[2,64,1024]{2,1,0:T(8,128)(2,1)S(1)}, bf16[2,64,1024]{2,1,0:T(8,128)(2,1)S(1)}, u32[]{:S(2)}, u32[]{:S(2)}) collective-permute-start(bf16[2,64,1024]{2,1,0:T(8,128)(2,1)S(1)} %broadcast_select_fusion), channel_id=1, source_target_pairs={{0,32},{1,97},{16,48},{17,113},{32,64},{33,1},{48,80},{49,17},{64,... | collective-permute-start | bytes 786440 | tf_op jit(solution)/shard_map/ppermute | solution.py:31
  135.9 32.4 %all-to-all-start.2 = ((bf16[32,32,384]{2,1,0:T(8,128)(2,1)}), bf16[32,32,384]{2,1,0:T(8,128)(2,1)}, u32[]{:S(2)}, u32[]{:S(2)}) async-start(bf16[32,32,384]{2,1,0:T(8,128)(2,1)} %bitcast.7), calls=%async_computation.2 | async-start | bytes 1572864 | tf_op jit(solution)/shard_map/all_to_all | solution.py:206
  146.2 10.5 %collective-permute-start.1 = (bf16[2,64,1024]{2,1,0:T(8,128)(2,1)S(1)}, bf16[2,64,1024]{2,1,0:T(8,128)(2,1)S(1)}, u32[]{:S(2)}, u32[]{:S(2)}) collective-permute-start(bf16[2,64,1024]{2,1,0:T(8,128)(2,1)S(1)} %attend.1.refs_1_), channel_id=1, source_target_pairs={{0,16},{16,32},{32,48},{48,64},{64,80},{80,96},{96,112},{112,0},{1... | collective-permute-start | bytes 786440 | tf_op jit(solution)/shard_map/ppermute | solution.py:26
  148.1 11.5 %collective-permute-start.2 = (bf16[2,64,1024]{2,1,0:T(8,128)(2,1)S(1)}, bf16[2,64,1024]{2,1,0:T(8,128)(2,1)S(1)}, u32[]{:S(2)}, u32[]{:S(2)}) collective-permute-start(bf16[2,64,1024]{2,1,0:T(8,128)(2,1)S(1)} %attend.1.refs_1_), channel_id=1, source_target_pairs={{0,112},{16,0},{32,16},{48,32},{64,48},{80,64},{96,80},{112,96},{1... | collective-permute-start | bytes 786440 | tf_op jit(solution)/shard_map/ppermute | solution.py:26
  159.6 1.0 copy-start.2
  160.6 0.9 copy-start.4
  161.5 0.9 copy-start.6
  168.4 42.7 %copy-start.9 = (s32[64]{0:T(128)S(1)}, s32[64]{0:T(128)}, u32[]{:S(2)}) copy-start(s32[64]{0:T(128)} %group_ref.1) | copy-start | bytes 772
  168.4 42.7 %copy-start.10 = (s32[64]{0:T(128)S(1)}, s32[64]{0:T(128)}, u32[]{:S(2)}) copy-start(s32[64]{0:T(128)} %first_ref.1) | copy-start | bytes 772

commit v2 on v1

--- a/solution.py
+++ b/solution.py
@@ -121,7 +121,7 @@
         acc = acc.astype(BF16).T.reshape(NZ, 2, 32, width)
         at = lax.rem(s_ref[0] + step + NX, NX)
         for half in range(2):
-            o_ref[at, :, :, half * width : (half + 1) * width] = acc[:, half]
+            o_ref[:, at, :, half * width : (half + 1) * width] = acc[:, half]
 
 
 def project(ids, rows, weights):
@@ -130,7 +130,7 @@
         lambda *refs: project_kernel(count, *refs),
         in_specs=[SMEM] + [VMEM] * (count + 8),
         out_specs=VMEM,
-        out_shape=pltpu.VMEM((NX, NZ, 32, 2 * count * DRAFT), BF16),
+        out_shape=pltpu.VMEM((NZ, NX, 32, 2 * count * DRAFT), BF16),
         compiler_params=PARAMS,
         name="project",
     )(ids, *map(near, rows), *map(near, weights))
@@ -145,9 +145,9 @@
         for slots, ref in zip(CHUNKS, parts):
             width = len(slots) * DRAFT
             for tile in range(2 * width // 128):
-                slab = ref[x, 0, :, tile * 128 : (tile + 1) * 128].astype(F32)
+                slab = ref[0, x, :, tile * 128 : (tile + 1) * 128].astype(F32)
                 for z in range(1, NZ):
-                    slab = slab + ref[x, z, :, tile * 128 : (tile + 1) * 128].astype(F32)
+                    slab = slab + ref[z, x, :, tile * 128 : (tile + 1) * 128].astype(F32)
                 for part in range(2):
                     column, at = divmod(2 * tile + part, len(slots))
                     request = (x * NY + lax.rem(my_y + slots[at] + NY, NY)) * 2 + core
@@ -242,7 +242,7 @@
     for slots in CHUNKS:
         part = project(ids, [arrived[s] for s in slots], weights)
         part = part.reshape(NX * NZ, 32, -1)
-        sums.append(exchange(part, ("x", "z")).reshape(NX, NZ, 32, -1))
+        sums.append(exchange(part, ("z", "x")).reshape(NZ, NX, 32, -1))
     placed = place([ids, draft_lengths, dest_group, dest_offset], sums)
     return finish(exchange(placed, ("z", "c")))
 

time: 235 us -> 234 us (level)
  no operation moved by 1% of the time
where the time goes in v2:
time: 234 us
  starting transfers between devices  95.1 us (41%)
  blocking collectives  62.4 us (27%)
  waiting for transfers between devices  49.8 us (21%)
  Pallas kernels  22.2 us (9%)
  local copies, waits for them, and re-layouts  3.56 us (2%)
    ppermute x13, starting transfers between devices, shift(): lax.ppermute(value, axis, [(i, (i + step) % size) for i in range(size)])  64.3 us
    all_to_all x2, blocking collectives, exchange(): return lax.all_to_all(value, axes, 0, 0, tiled=True)  62.4 us
    ppermute x13, waiting for transfers between devices, shift(): lax.ppermute(value, axis, [(i, (i + step) % size) for i in range(size)])  41.7 us
    all_to_all x2, starting transfers between devices, exchange(): return lax.all_to_all(value, axes, 0, 0, tiled=True)  22.2 us
    pallas_call x2, Pallas kernels, project(): pl.pallas_call(lambda *refs: project_kernel(count, *refs), in_specs=[SMEM...  11.6 us
    ppermute x2, starting transfers between devices, shift_cores(): return lax.ppermute(value, (axis, 'c'), pairs)  8.55 us
    ppermute x2, waiting for transfers between devices, shift_cores(): return lax.ppermute(value, (axis, 'c'), pairs)  8.13 us
    pallas_call x1, Pallas kernels, attend(): pl.pallas_call(attend_kernel, grid_spec=pltpu.PrefetchScalarGridSpec(num_...  5.87 us
  transfers between devices with their start and end apart: 17, of which 7 were waited for; matrix products, arithmetic and copies ran while one was open for 0% of the time, Pallas kernels for 5%

profile of v2, /device:TPU:1, one launch (start us, length us, event | category | flops | bytes accessed | tf_op | source)
XLA Modules:
  0.0 233.5 jit_solution(11035388812258755393)
XLA Ops:
  0.0 2.1 pack_kv.1
  2.1 0.0 copy-start.8
  2.1 12.0 %all-to-all-start = ((bf16[16,2,128,128]{3,2,1,0:T(8,128)(2,1)}), bf16[16,2,128,128]{3,2,1,0:T(8,128)(2,1)S(1)}, u32[]{:S(2)}, u32[]{:S(2)}) async-start(bf16[16,2,128,128]{3,2,1,0:T(8,128)(2,1)} %bitcast.4), calls=%async_computation | async-start | bytes 2097152 | tf_op jit(solution)/shard_map/all_to_all | solution.py:206
  14.1 3.1 %collective-permute-start.6 = (bf16[1024,512]{1,0:T(8,128)(2,1)S(1)}, bf16[1024,512]{1,0:T(8,128)(2,1)S(1)}, u32[]{:S(2)}, u32[]{:S(2)}) collective-permute-start(bf16[1024,512]{1,0:T(8,128)(2,1)S(1)} %copy-done), channel_id=1, source_target_pairs={{0,128},{128,256},{256,384},{384,0},{1,129},{129,257},{257,385},{3... | collective-permute-start | bytes 3145736 | tf_op jit(solution)/shard_map/ppermute | solution.py:26
  17.2 3.4 %collective-permute-start.8 = (bf16[1024,512]{1,0:T(8,128)(2,1)S(1)}, bf16[1024,512]{1,0:T(8,128)(2,1)}, u32[]{:S(2)}, u32[]{:S(2)}) collective-permute-start(bf16[1024,512]{1,0:T(8,128)(2,1)S(1)} %copy-done), channel_id=1, source_target_pairs={{0,384},{128,0},{256,128},{384,256},{1,385},{129,1},{257,129},{385... | collective-permute-start | bytes 3145736 | tf_op jit(solution)/shard_map/ppermute | solution.py:26
  20.6 3.4 %collective-permute-start.10 = (bf16[1024,512]{1,0:T(8,128)(2,1)S(1)}, bf16[1024,512]{1,0:T(8,128)(2,1)}, u32[]{:S(2)}, u32[]{:S(2)}) collective-permute-start(bf16[1024,512]{1,0:T(8,128)(2,1)S(1)} %copy-done), channel_id=1, source_target_pairs={{0,256},{1,257},{128,384},{129,385},{256,0},{257,1},{384,128},{385... | collective-permute-start | bytes 3145736 | tf_op jit(solution)/shard_map/ppermute | solution.py:31
  24.0 2.9 %collective-permute-start.5 = (bf16[1024,512]{1,0:T(8,128)(2,1)S(1)}, bf16[1024,512]{1,0:T(8,128)(2,1)}, u32[]{:S(2)}, u32[]{:S(2)}) collective-permute-start(bf16[1024,512]{1,0:T(8,128)(2,1)S(1)} %copy-done), channel_id=1, source_target_pairs={{0,1},{1,0},{2,3},{3,2},{4,5},{5,4},{6,7},{7,6},{8,9},{9,8},{10,11... | collective-permute-start | bytes 3145736 | tf_op jit(solution)/shard_map/ppermute | solution.py:26
  26.9 14.9 %collective-permute-done.6.refs_8_.refs_6_ = bf16[1024,512]{1,0:T(8,128)(2,1)S(1)} collective-permute-done((bf16[1024,512]{1,0:T(8,128)(2,1)S(1)}, bf16[1024,512]{1,0:T(8,128)(2,1)S(1)}, u32[]{:S(2)}, u32[]{:S(2)}) %collective-permute-start.6) | collective-permute-done | bytes 1048608 | tf_op jit(solution)/shard_map/ppermute | solution.py:26
  41.8 2.9 %collective-permute-start.7 = (bf16[1024,512]{1,0:T(8,128)(2,1)S(1)}, bf16[1024,512]{1,0:T(8,128)(2,1)}, u32[]{:S(2)}, u32[]{:S(2)}) collective-permute-start(bf16[1024,512]{1,0:T(8,128)(2,1)S(1)} %collective-permute-done.6.refs_8_.refs_6_), channel_id=1, source_target_pairs={{0,1},{1,0},{2,3},{3,2},{4,5},{5,4},{6,7},{7,6},{8,9},{9,8},{10,11... | collective-permute-start | bytes 3145736 | tf_op jit(solution)/shard_map/ppermute | solution.py:26
  44.7 0.7 constant_dynamic-slice_fusion
  45.4 1.9 collective-permute-start
  47.3 0.0 collective-permute-done.8.refs_10_.refs_8_
  47.3 21.1 %collective-permute-start.9 = (bf16[1024,512]{1,0:T(8,128)(2,1)}, bf16[1024,512]{1,0:T(8,128)(2,1)}, u32[]{:S(2)}, u32[]{:S(2)}) collective-permute-start(bf16[1024,512]{1,0:T(8,128)(2,1)} %collective-permute-done.8.refs_10_.refs_8_), channel_id=1, source_target_pairs={{0,1},{1,0},{2,3},{3,2},{4,5},{5,4},{6,7},{7,6},{8,9},{9,8},{10,11... | collective-permute-start | bytes 3145736 | tf_op jit(solution)/shard_map/ppermute | solution.py:26
  68.4 0.0 collective-permute-done.10.refs_12_.refs_10_
  68.4 1.9 collective-permute-start.11
  70.3 0.1 pad_add_fusion.s_ref.refs_0_
  70.4 0.0 collective-permute-done.other_ref
  70.4 0.0 all-to-all-done.kv_ref
  70.4 5.9 %attend.1.refs_1_ = bf16[2,64,1024]{2,1,0:T(8,128)(2,1)S(1)} custom-call(s32[4]{0:T(128)S(1)} %pad_add_fusion.s_ref.refs_0_, s32[2]{0:T(128)S(1)} %copy-done.8, s32[64]{0:T(128)S(1)} %copy-done.7, bf16[128,1024]{1,0:T(8,128)(2,1)} %mine_ref.1, bf16[64,1024]{1,0:T(8,128)(2,1)S(1)} %collective-permute-done.other_ref, ...), custom_call_target="tpu_custom_call" | custom-call | tf_op jit(solution)/shard_map/attend/pallas_call | solution.py:93
  76.3 4.2 %collective-permute-start.3 = (bf16[2,64,1024]{2,1,0:T(8,128)(2,1)S(1)}, bf16[2,64,1024]{2,1,0:T(8,128)(2,1)S(1)}, u32[]{:S(2)}, u32[]{:S(2)}) collective-permute-start(bf16[2,64,1024]{2,1,0:T(8,128)(2,1)S(1)} %attend.1.refs_1_), channel_id=1, source_target_pairs={{0,32},{16,48},{32,64},{48,80},{64,96},{80,112},{96,0},{112,16},{1... | collective-permute-start | bytes 786440 | tf_op jit(solution)/shard_map/ppermute | solution.py:26
  80.5 10.8 %collective-permute-done.3.refs_4_ = bf16[2,64,1024]{2,1,0:T(8,128)(2,1)S(1)} collective-permute-done((bf16[2,64,1024]{2,1,0:T(8,128)(2,1)S(1)}, bf16[2,64,1024]{2,1,0:T(8,128)(2,1)S(1)}, u32[]{:S(2)}, u32[]{:S(2)}) %collective-permute-start.3) | collective-permute-done | bytes 262176 | tf_op jit(solution)/shard_map/ppermute | solution.py:26
  91.3 3.1 %collective-permute-start.4 = (bf16[2,64,1024]{2,1,0:T(8,128)(2,1)S(1)}, bf16[2,64,1024]{2,1,0:T(8,128)(2,1)S(1)}, u32[]{:S(2)}, u32[]{:S(2)}) collective-permute-start(bf16[2,64,1024]{2,1,0:T(8,128)(2,1)S(1)} %attend.1.refs_1_), channel_id=1, source_target_pairs={{0,96},{16,112},{32,0},{48,16},{64,32},{80,48},{96,64},{112,80},{1... | collective-permute-start | bytes 786440 | tf_op jit(solution)/shard_map/ppermute | solution.py:26
  94.4 5.5 %collective-permute-done.4.refs_5_ = bf16[2,64,1024]{2,1,0:T(8,128)(2,1)S(1)} collective-permute-done((bf16[2,64,1024]{2,1,0:T(8,128)(2,1)S(1)}, bf16[2,64,1024]{2,1,0:T(8,128)(2,1)S(1)}, u32[]{:S(2)}, u32[]{:S(2)}) %collective-permute-start.4) | collective-permute-done | bytes 262176 | tf_op jit(solution)/shard_map/ppermute | solution.py:26
  99.9 9.2 %collective-permute-start.12 = (bf16[2,64,1024]{2,1,0:T(8,128)(2,1)S(1)}, bf16[2,64,1024]{2,1,0:T(8,128)(2,1)S(1)}, u32[]{:S(2)}, u32[]{:S(2)}) collective-permute-start(bf16[2,64,1024]{2,1,0:T(8,128)(2,1)S(1)} %collective-permute-done.3.refs_4_), channel_id=1, source_target_pairs={{0,16},{16,32},{32,48},{48,64},{64,80},{80,96},{96,112},{112,0},{1... | collective-permute-start | bytes 786440 | tf_op jit(solution)/shard_map/ppermute | solution.py:26
  109.2 0.0 collective-permute-done.5.refs_7_.refs_5_
  109.2 4.2 %collective-permute-start.13 = (bf16[2,64,1024]{2,1,0:T(8,128)(2,1)S(1)}, bf16[2,64,1024]{2,1,0:T(8,128)(2,1)S(1)}, u32[]{:S(2)}, u32[]{:S(2)}) collective-permute-start(bf16[2,64,1024]{2,1,0:T(8,128)(2,1)S(1)} %collective-permute-done.4.refs_5_), channel_id=1, source_target_pairs={{0,112},{16,0},{32,16},{48,32},{64,48},{80,64},{96,80},{112,96},{1... | collective-permute-start | bytes 786440 | tf_op jit(solution)/shard_map/ppermute | solution.py:26
  113.4 0.0 collective-permute-done.7.refs_9_.refs_7_
  113.4 5.1 %collective-permute-start.14 = (bf16[2,64,1024]{2,1,0:T(8,128)(2,1)S(1)}, bf16[2,64,1024]{2,1,0:T(8,128)(2,1)S(1)}, u32[]{:S(2)}, u32[]{:S(2)}) collective-permute-start(bf16[2,64,1024]{2,1,0:T(8,128)(2,1)S(1)} %broadcast_select_fusion), channel_id=1, source_target_pairs={{0,32},{1,97},{16,48},{17,113},{32,64},{33,1},{48,80},{49,17},{64,... | collective-permute-start | bytes 786440 | tf_op jit(solution)/shard_map/ppermute | solution.py:31
  118.5 0.0 collective-permute-done.9.refs_11_.refs_9_
  118.5 3.5 %collective-permute-done.13.refs_2_ = bf16[2,64,1024]{2,1,0:T(8,128)(2,1)S(1)} collective-permute-done((bf16[2,64,1024]{2,1,0:T(8,128)(2,1)S(1)}, bf16[2,64,1024]{2,1,0:T(8,128)(2,1)S(1)}, u32[]{:S(2)}, u32[]{:S(2)}) %collective-permute-start.13) | collective-permute-done | bytes 262176 | tf_op jit(solution)/shard_map/ppermute | solution.py:26
  122.1 8.1 %collective-permute-done.14.refs_3_ = bf16[2,64,1024]{2,1,0:T(8,128)(2,1)S(1)} collective-permute-done((bf16[2,64,1024]{2,1,0:T(8,128)(2,1)S(1)}, bf16[2,64,1024]{2,1,0:T(8,128)(2,1)S(1)}, u32[]{:S(2)}, u32[]{:S(2)}) %collective-permute-start.14) | collective-permute-done | bytes 262176 | tf_op jit(solution)/shard_map/ppermute | solution.py:31
  130.2 5.7 %project.3 = bf16[8,4,32,384]{3,2,1,0:T(8,128)(2,1)} custom-call(s32[4]{0:T(128)S(1)} %pad_add_fusion.s_ref.refs_0_, bf16[2,64,1024]{2,1,0:T(8,128)(2,1)S(1)} %collective-permute-done.12.refs_1_, bf16[2,64,1024]{2,1,0:T(8,128)(2,1)S(1)} %collective-permute-done.13.refs_2_, bf16[2,64,1024]{2,1,0:T(8,128)(2,1)S(1)} %collective-permute-done.14.refs_3_, ...), custom_call_target="tpu_custom_call" | custom-call | tf_op jit(solution)/shard_map/project/pallas_call | solution.py:129
  135.9 10.3 %all-to-all-start.2 = ((bf16[32,32,384]{2,1,0:T(8,128)(2,1)}), bf16[32,32,384]{2,1,0:T(8,128)(2,1)}, u32[]{:S(2)}, u32[]{:S(2)}) async-start(bf16[32,32,384]{2,1,0:T(8,128)(2,1)} %bitcast.7), calls=%async_computation.2 | async-start | bytes 1572864 | tf_op jit(solution)/shard_map/all_to_all | solution.py:206
  146.2 1.9 collective-permute-start.1
  148.1 4.6 %collective-permute-start.2 = (bf16[2,64,1024]{2,1,0:T(8,128)(2,1)S(1)}, bf16[2,64,1024]{2,1,0:T(8,128)(2,1)S(1)}, u32[]{:S(2)}, u32[]{:S(2)}) collective-permute-start(bf16[2,64,1024]{2,1,0:T(8,128)(2,1)S(1)} %attend.1.refs_1_), channel_id=1, source_target_pairs={{0,112},{16,0},{32,16},{48,32},{64,48},{80,64},{96,80},{112,96},{1... | collective-permute-start | bytes 786440 | tf_op jit(solution)/shard_map/ppermute | solution.py:26
  152.7 4.1 %collective-permute-done.1.refs_2_ = bf16[2,64,1024]{2,1,0:T(8,128)(2,1)S(1)} collective-permute-done((bf16[2,64,1024]{2,1,0:T(8,128)(2,1)S(1)}, bf16[2,64,1024]{2,1,0:T(8,128)(2,1)S(1)}, u32[]{:S(2)}, u32[]{:S(2)}) %collective-permute-start.1) | collective-permute-done | bytes 262176 | tf_op jit(solution)/shard_map/ppermute | solution.py:26
  156.8 2.8 %collective-permute-done.2.refs_3_ = bf16[2,64,1024]{2,1,0:T(8,128)(2,1)S(1)} collective-permute-done((bf16[2,64,1024]{2,1,0:T(8,128)(2,1)S(1)}, bf16[2,64,1024]{2,1,0:T(8,128)(2,1)S(1)}, u32[]{:S(2)}, u32[]{:S(2)}) %collective-permute-start.2) | collective-permute-done | bytes 262176 | tf_op jit(solution)/shard_map/ppermute | solution.py:26
  159.6 0.9 copy-done.2
  160.6 0.9 copy-done.4
  161.5 0.9 copy-done.6
  162.5 5.9 %project.2 = bf16[8,4,32,640]{3,2,1,0:T(8,128)(2,1)S(1)} custom-call(s32[4]{0:T(128)S(1)} %pad_add_fusion.s_ref.refs_0_, bf16[2,64,1024]{2,1,0:T(8,128)(2,1)S(1)} %copy-done.2, bf16[2,64,1024]{2,1,0:T(8,128)(2,1)S(1)} %collective-permute-done.1.refs_2_, bf16[2,64,1024]{2,1,0:T(8,128)(2,1)S(1)} %collective-permute-done.2.refs_3_, ...), custom_call_target="tpu_custom_call" | custom-call | tf_op jit(solution)/shard_map/project/pallas_call | solution.py:129
  168.4 0.0 all-to-all-done.2
  168.4 0.0 copy-start.9
  168.4 0.0 copy-start.10
  168.4 44.1 %all_to_all.20 = bf16[32,32,640]{2,1,0:T(8,128)(2,1)S(1)} all-to-all(bf16[32,32,640]{2,1,0:T(8,128)(2,1)S(1)} %bitcast.10), channel_id=1, replica_groups=mesh['x'=4,'y'=8,'z'=8,'c'=2] {'z','x'}, dimensions={0} | all-to-all | bytes 2621440 | tf_op jit(solution)/shard_map/all_to_all | solution.py:206
  212.5 1.8 place.1
  214.3 18.3 %all_to_all.21.i_ref = bf16[16,32,384]{2,1,0:T(8,128)(2,1)S(1)} all-to-all(bf16[16,32,384]{2,1,0:T(8,128)(2,1)S(1)} %place.1), channel_id=1, replica_groups=mesh['x'=4,'y'=8,'z'=8,'c'=2] {'z','c'}, dimensions={0} | all-to-all | bytes 786432 | tf_op jit(solution)/shard_map/all_to_all | solution.py:206
  232.6 0.9 finish.1
  (21 shorter events, 0.1 us)
Async XLA Ops:
  2.1 12.0 %copy-start = (bf16[1024,512]{1,0:T(8,128)(2,1)S(1)}, bf16[1024,512]{1,0:T(8,128)(2,1)}, u32[]{:S(2)}) copy-start(bf16[1024,512]{1,0:T(8,128)(2,1)} %refs_4_.1) | copy-start | bytes 3145732
  2.1 42.6 %copy-start.11 = (bf16[128,1024]{1,0:T(8,128)(2,1)S(1)}, bf16[128,1024]{1,0:T(8,128)(2,1)}, u32[]{:S(2)}) copy-start(bf16[128,1024]{1,0:T(8,128)(2,1)} %mine_ref.1) | copy-start | bytes 786436
  2.1 68.3 %copy-start.7 = (s32[64]{0:T(128)S(1)}, s32[64]{0:T(128)}, u32[]{:S(2)}) copy-start(s32[64]{0:T(128)} %length_ref.1) | copy-start | bytes 772
  2.1 68.3 %copy-start.8 = (s32[2]{0:T(128)S(1)}, s32[2]{0:T(128)}, u32[]{:S(2)}) copy-start(s32[2]{0:T(128)} %cache_ref.1) | copy-start | bytes 28
  2.1 68.3 %all-to-all-start = ((bf16[16,2,128,128]{3,2,1,0:T(8,128)(2,1)}), bf16[16,2,128,128]{3,2,1,0:T(8,128)(2,1)S(1)}, u32[]{:S(2)}, u32[]{:S(2)}) async-start(bf16[16,2,128,128]{3,2,1,0:T(8,128)(2,1)} %bitcast.4), calls=%async_computation | async-start | bytes 2097152 | tf_op jit(solution)/shard_map/all_to_all | solution.py:206
  14.1 27.7 %collective-permute-start.6 = (bf16[1024,512]{1,0:T(8,128)(2,1)S(1)}, bf16[1024,512]{1,0:T(8,128)(2,1)S(1)}, u32[]{:S(2)}, u32[]{:S(2)}) collective-permute-start(bf16[1024,512]{1,0:T(8,128)(2,1)S(1)} %copy-done), channel_id=1, source_target_pairs={{0,128},{128,256},{256,384},{384,0},{1,129},{129,257},{257,385},{3... | collective-permute-start | bytes 3145736 | tf_op jit(solution)/shard_map/ppermute | solution.py:26
  17.2 30.1 %collective-permute-start.8 = (bf16[1024,512]{1,0:T(8,128)(2,1)S(1)}, bf16[1024,512]{1,0:T(8,128)(2,1)}, u32[]{:S(2)}, u32[]{:S(2)}) collective-permute-start(bf16[1024,512]{1,0:T(8,128)(2,1)S(1)} %copy-done), channel_id=1, source_target_pairs={{0,384},{128,0},{256,128},{384,256},{1,385},{129,1},{257,129},{385... | collective-permute-start | bytes 3145736 | tf_op jit(solution)/shard_map/ppermute | solution.py:26
  20.6 47.8 %collective-permute-start.10 = (bf16[1024,512]{1,0:T(8,128)(2,1)S(1)}, bf16[1024,512]{1,0:T(8,128)(2,1)}, u32[]{:S(2)}, u32[]{:S(2)}) collective-permute-start(bf16[1024,512]{1,0:T(8,128)(2,1)S(1)} %copy-done), channel_id=1, source_target_pairs={{0,256},{1,257},{128,384},{129,385},{256,0},{257,1},{384,128},{385... | collective-permute-start | bytes 3145736 | tf_op jit(solution)/shard_map/ppermute | solution.py:31
  24.0 85.2 %collective-permute-start.5 = (bf16[1024,512]{1,0:T(8,128)(2,1)S(1)}, bf16[1024,512]{1,0:T(8,128)(2,1)}, u32[]{:S(2)}, u32[]{:S(2)}) collective-permute-start(bf16[1024,512]{1,0:T(8,128)(2,1)S(1)} %copy-done), channel_id=1, source_target_pairs={{0,1},{1,0},{2,3},{3,2},{4,5},{5,4},{6,7},{7,6},{8,9},{9,8},{10,11... | collective-permute-start | bytes 3145736 | tf_op jit(solution)/shard_map/ppermute | solution.py:26
  41.8 71.6 %collective-permute-start.7 = (bf16[1024,512]{1,0:T(8,128)(2,1)S(1)}, bf16[1024,512]{1,0:T(8,128)(2,1)}, u32[]{:S(2)}, u32[]{:S(2)}) collective-permute-start(bf16[1024,512]{1,0:T(8,128)(2,1)S(1)} %collective-permute-done.6.refs_8_.refs_6_), channel_id=1, source_target_pairs={{0,1},{1,0},{2,3},{3,2},{4,5},{5,4},{6,7},{7,6},{8,9},{9,8},{10,11... | collective-permute-start | bytes 3145736 | tf_op jit(solution)/shard_map/ppermute | solution.py:26
  45.4 25.0 %collective-permute-start = (bf16[64,1024]{1,0:T(8,128)(2,1)}, bf16[64,1024]{1,0:T(8,128)(2,1)S(1)}, u32[]{:S(2)}, u32[]{:S(2)}) collective-permute-start(bf16[64,1024]{1,0:T(8,128)(2,1)} %constant_dynamic-slice_fusion), channel_id=1, source_target_pairs={{0,1},{1,0},{2,3},{3,2},{4,5},{5,4},{6,7},{7,6},{8,9},{9,8},{10,11... | collective-permute-start | bytes 393224 | tf_op jit(solution)/shard_map/ppermute | solution.py:26
  47.3 71.2 %collective-permute-start.9 = (bf16[1024,512]{1,0:T(8,128)(2,1)}, bf16[1024,512]{1,0:T(8,128)(2,1)}, u32[]{:S(2)}, u32[]{:S(2)}) collective-permute-start(bf16[1024,512]{1,0:T(8,128)(2,1)} %collective-permute-done.8.refs_10_.refs_8_), channel_id=1, source_target_pairs={{0,1},{1,0},{2,3},{3,2},{4,5},{5,4},{6,7},{7,6},{8,9},{9,8},{10,11... | collective-permute-start | bytes 3145736 | tf_op jit(solution)/shard_map/ppermute | solution.py:26
  68.4 50.2 %collective-permute-start.11 = (bf16[1024,512]{1,0:T(8,128)(2,1)}, bf16[1024,512]{1,0:T(8,128)(2,1)}, u32[]{:S(2)}, u32[]{:S(2)}) collective-permute-start(bf16[1024,512]{1,0:T(8,128)(2,1)} %collective-permute-done.10.refs_12_.refs_10_), channel_id=1, source_target_pairs={{0,1},{1,0},{2,3},{3,2},{4,5},{5,4},{6,7},{7,6},{8,9},{9,8},{10,11... | collective-permute-start | bytes 3145736 | tf_op jit(solution)/shard_map/ppermute | solution.py:26
  76.3 71.8 %copy-start.1 = (bf16[2,64,1024]{2,1,0:T(8,128)(2,1)}, bf16[2,64,1024]{2,1,0:T(8,128)(2,1)S(1)}, u32[]{:S(2)}) copy-start(bf16[2,64,1024]{2,1,0:T(8,128)(2,1)S(1)} %attend.1.refs_1_) | copy-start | bytes 786436
  76.3 15.0 %collective-permute-start.3 = (bf16[2,64,1024]{2,1,0:T(8,128)(2,1)S(1)}, bf16[2,64,1024]{2,1,0:T(8,128)(2,1)S(1)}, u32[]{:S(2)}, u32[]{:S(2)}) collective-permute-start(bf16[2,64,1024]{2,1,0:T(8,128)(2,1)S(1)} %attend.1.refs_1_), channel_id=1, source_target_pairs={{0,32},{16,48},{32,64},{48,80},{64,96},{80,112},{96,0},{112,16},{1... | collective-permute-start | bytes 786440 | tf_op jit(solution)/shard_map/ppermute | solution.py:26
  91.3 44.6 %copy-start.3 = (bf16[2,64,1024]{2,1,0:T(8,128)(2,1)}, bf16[2,64,1024]{2,1,0:T(8,128)(2,1)S(1)}, u32[]{:S(2)}) copy-start(bf16[2,64,1024]{2,1,0:T(8,128)(2,1)S(1)} %collective-permute-done.3.refs_4_) | copy-start | bytes 786436
  91.3 8.6 %collective-permute-start.4 = (bf16[2,64,1024]{2,1,0:T(8,128)(2,1)S(1)}, bf16[2,64,1024]{2,1,0:T(8,128)(2,1)S(1)}, u32[]{:S(2)}, u32[]{:S(2)}) collective-permute-start(bf16[2,64,1024]{2,1,0:T(8,128)(2,1)S(1)} %attend.1.refs_1_), channel_id=1, source_target_pairs={{0,96},{16,112},{32,0},{48,16},{64,32},{80,48},{96,64},{112,80},{1... | collective-permute-start | bytes 786440 | tf_op jit(solution)/shard_map/ppermute | solution.py:26
  99.9 36.0 %copy-start.5 = (bf16[2,64,1024]{2,1,0:T(8,128)(2,1)}, bf16[2,64,1024]{2,1,0:T(8,128)(2,1)S(1)}, u32[]{:S(2)}) copy-start(bf16[2,64,1024]{2,1,0:T(8,128)(2,1)S(1)} %collective-permute-done.4.refs_5_) | copy-start | bytes 786436
  99.9 18.6 %collective-permute-start.12 = (bf16[2,64,1024]{2,1,0:T(8,128)(2,1)S(1)}, bf16[2,64,1024]{2,1,0:T(8,128)(2,1)S(1)}, u32[]{:S(2)}, u32[]{:S(2)}) collective-permute-start(bf16[2,64,1024]{2,1,0:T(8,128)(2,1)S(1)} %collective-permute-done.3.refs_4_), channel_id=1, source_target_pairs={{0,16},{16,32},{32,48},{48,64},{64,80},{80,96},{96,112},{112,0},{1... | collective-permute-start | bytes 786440 | tf_op jit(solution)/shard_map/ppermute | solution.py:26
  109.2 12.9 %collective-permute-start.13 = (bf16[2,64,1024]{2,1,0:T(8,128)(2,1)S(1)}, bf16[2,64,1024]{2,1,0:T(8,128)(2,1)S(1)}, u32[]{:S(2)}, u32[]{:S(2)}) collective-permute-start(bf16[2,64,1024]{2,1,0:T(8,128)(2,1)S(1)} %collective-permute-done.4.refs_5_), channel_id=1, source_target_pairs={{0,112},{16,0},{32,16},{48,32},{64,48},{80,64},{96,80},{112,96},{1... | collective-permute-start | bytes 786440 | tf_op jit(solution)/shard_map/ppermute | solution.py:26
  113.4 16.8 %collective-permute-start.14 = (bf16[2,64,1024]{2,1,0:T(8,128)(2,1)S(1)}, bf16[2,64,1024]{2,1,0:T(8,128)(2,1)S(1)}, u32[]{:S(2)}, u32[]{:S(2)}) collective-permute-start(bf16[2,64,1024]{2,1,0:T(8,128)(2,1)S(1)} %broadcast_select_fusion), channel_id=1, source_target_pairs={{0,32},{1,97},{16,48},{17,113},{32,64},{33,1},{48,80},{49,17},{64,... | collective-permute-start | bytes 786440 | tf_op jit(solution)/shard_map/ppermute | solution.py:31
  135.9 32.4 %all-to-all-start.2 = ((bf16[32,32,384]{2,1,0:T(8,128)(2,1)}), bf16[32,32,384]{2,1,0:T(8,128)(2,1)}, u32[]{:S(2)}, u32[]{:S(2)}) async-start(bf16[32,32,384]{2,1,0:T(8,128)(2,1)} %bitcast.7), calls=%async_computation.2 | async-start | bytes 1572864 | tf_op jit(solution)/shard_map/all_to_all | solution.py:206
  146.2 10.6 %collective-permute-start.1 = (bf16[2,64,1024]{2,1,0:T(8,128)(2,1)S(1)}, bf16[2,64,1024]{2,1,0:T(8,128)(2,1)S(1)}, u32[]{:S(2)}, u32[]{:S(2)}) collective-permute-start(bf16[2,64,1024]{2,1,0:T(8,128)(2,1)S(1)} %attend.1.refs_1_), channel_id=1, source_target_pairs={{0,16},{16,32},{32,48},{48,64},{64,80},{80,96},{96,112},{112,0},{1... | collective-permute-start | bytes 786440 | tf_op jit(solution)/shard_map/ppermute | solution.py:26
  148.1 11.5 %collective-permute-start.2 = (bf16[2,64,1024]{2,1,0:T(8,128)(2,1)S(1)}, bf16[2,64,1024]{2,1,0:T(8,128)(2,1)S(1)}, u32[]{:S(2)}, u32[]{:S(2)}) collective-permute-start(bf16[2,64,1024]{2,1,0:T(8,128)(2,1)S(1)} %attend.1.refs_1_), channel_id=1, source_target_pairs={{0,112},{16,0},{32,16},{48,32},{64,48},{80,64},{96,80},{112,96},{1... | collective-permute-start | bytes 786440 | tf_op jit(solution)/shard_map/ppermute | solution.py:26
  159.6 1.0 copy-start.2
  160.6 0.9 copy-start.4
  161.5 0.9 copy-start.6
  168.4 44.2 %copy-start.9 = (s32[64]{0:T(128)S(1)}, s32[64]{0:T(128)}, u32[]{:S(2)}) copy-start(s32[64]{0:T(128)} %group_ref.1) | copy-start | bytes 772
  168.4 44.2 %copy-start.10 = (s32[64]{0:T(128)S(1)}, s32[64]{0:T(128)}, u32[]{:S(2)}) copy-start(s32[64]{0:T(128)} %first_ref.1) | copy-start | bytes 772

commit v3 on v2

--- a/solution.py
+++ b/solution.py
@@ -69,8 +69,10 @@
     slot = lax.broadcasted_iota(jnp.int32, (256, DRAFT), 1)
     keep_draft = (slot <= row) & (slot < draft_len)
     live = lax.broadcasted_iota(jnp.int32, (256, 1), 0) % DRAFT < draft_len
-    for side, q_ref in enumerate((mine_ref, other_ref)):
-        q = jnp.concatenate([q_ref[:, h * HEAD_DIM : (h + 1) * HEAD_DIM] for h in range(4)], axis=0)
+    for block in range(4):
+        side, q_ref = block // 2, (mine_ref, other_ref)[block // 2]
+        columns = [slice(h * HEAD_DIM, (h + 1) * HEAD_DIM) for h in range(4 * (block % 2), 4 * (block % 2) + 4)]
+        q = jnp.concatenate([q_ref[:, at] for at in columns], axis=0)
         cached = lax.dot_general(q, keys, NT, preferred_element_type=F32)
         drafted = lax.dot_general(q, dk, NT, preferred_element_type=F32)
         cached = jnp.where(keep, cached, NEG_FILL)
@@ -84,8 +86,8 @@
         mixed = jnp.dot(cached.astype(BF16), values, preferred_element_type=F32)
         mixed = mixed + jnp.dot(drafted.astype(BF16), dv, preferred_element_type=F32)
         mixed = jnp.where(live, mixed / total, 0.0).astype(BF16)
-        for h in range(4):
-            o_ref[side, :, h * HEAD_DIM : (h + 1) * HEAD_DIM] = mixed[h * DRAFT : (h + 1) * DRAFT]
+        for h, at in enumerate(columns):
+            o_ref[side, :, at] = mixed[h * DRAFT : (h + 1) * DRAFT]
 
 
 def attend(ids, cache_lengths, draft_lengths, q, other_q, kv, dk, dv):
@@ -94,15 +96,15 @@
         attend_kernel,
         grid_spec=pltpu.PrefetchScalarGridSpec(
             num_scalar_prefetch=3,
-            grid=(2,),
+            grid=(1,),
             in_specs=[
-                pl.BlockSpec((DRAFT, 512), lambda p, s, *_: (s[3], p)),
-                pl.BlockSpec((DRAFT, 512), lambda p, *_: (0, p)),
+                pl.BlockSpec((DRAFT, 1024), lambda p, s, *_: (s[3], p)),
+                pl.BlockSpec((DRAFT, 1024), lambda p, *_: (0, p)),
                 pl.BlockSpec((16, 2, 128, 128), lambda p, *_: (0, 0, 0, 0)),
                 draft,
                 draft,
             ],
-            out_specs=pl.BlockSpec((2, DRAFT, 512), lambda p, *_: (0, 0, p)),
+            out_specs=pl.BlockSpec((2, DRAFT, 1024), lambda p, *_: (0, 0, p)),
         ),
         out_shape=pltpu.VMEM((2, DRAFT, 1024), BF16),
         compiler_params=PARAMS,

time: 234 us -> 234 us (level)
  no operation moved by 1% of the time
where the time goes in v3:
time: 234 us; the launch traced here: 233 us
  starting transfers between devices  95 us (41%)
  blocking collectives  62.4 us (27%)
  waiting for transfers between devices  49.8 us (21%)
  Pallas kernels  21.8 us (9%)
  local copies, waits for them, and re-layouts  3.56 us (2%)
    ppermute x13, starting transfers between devices, shift(): lax.ppermute(value, axis, [(i, (i + step) % size) for i in range(size)])  64.3 us
    all_to_all x2, blocking collectives, exchange(): return lax.all_to_all(value, axes, 0, 0, tiled=True)  62.4 us
    ppermute x13, waiting for transfers between devices, shift(): lax.ppermute(value, axis, [(i, (i + step) % size) for i in range(size)])  41.7 us
    all_to_all x2, starting transfers between devices, exchange(): return lax.all_to_all(value, axes, 0, 0, tiled=True)  22.2 us
    pallas_call x2, Pallas kernels, project(): pl.pallas_call(lambda *refs: project_kernel(count, *refs), in_specs=[SMEM...  11.6 us
    ppermute x2, starting transfers between devices, shift_cores(): return lax.ppermute(value, (axis, 'c'), pairs)  8.55 us
    ppermute x2, waiting for transfers between devices, shift_cores(): return lax.ppermute(value, (axis, 'c'), pairs)  8.13 us
    pallas_call x1, Pallas kernels, attend(): pl.pallas_call(attend_kernel, grid_spec=pltpu.PrefetchScalarGridSpec(num_...  5.44 us
  transfers between devices with their start and end apart: 17, of which 7 were waited for; matrix products, arithmetic and copies ran while one was open for 0% of the time, Pallas kernels for 5%

profile of v3, /device:TPU:1, one launch (start us, length us, event | category | flops | bytes accessed | tf_op | source)
XLA Modules:
  0.0 233.1 jit_solution(13023516032902906453)
XLA Ops:
  0.0 2.1 pack_kv.1
  2.1 0.0 copy-start.8
  2.1 12.0 %all-to-all-start = ((bf16[16,2,128,128]{3,2,1,0:T(8,128)(2,1)}), bf16[16,2,128,128]{3,2,1,0:T(8,128)(2,1)S(1)}, u32[]{:S(2)}, u32[]{:S(2)}) async-start(bf16[16,2,128,128]{3,2,1,0:T(8,128)(2,1)} %bitcast.4), calls=%async_computation | async-start | bytes 2097152 | tf_op jit(solution)/shard_map/all_to_all | solution.py:208
  14.1 3.1 %collective-permute-start.6 = (bf16[1024,512]{1,0:T(8,128)(2,1)S(1)}, bf16[1024,512]{1,0:T(8,128)(2,1)S(1)}, u32[]{:S(2)}, u32[]{:S(2)}) collective-permute-start(bf16[1024,512]{1,0:T(8,128)(2,1)S(1)} %copy-done), channel_id=1, source_target_pairs={{0,128},{128,256},{256,384},{384,0},{1,129},{129,257},{257,385},{3... | collective-permute-start | bytes 3145736 | tf_op jit(solution)/shard_map/ppermute | solution.py:26
  17.2 3.4 %collective-permute-start.8 = (bf16[1024,512]{1,0:T(8,128)(2,1)S(1)}, bf16[1024,512]{1,0:T(8,128)(2,1)}, u32[]{:S(2)}, u32[]{:S(2)}) collective-permute-start(bf16[1024,512]{1,0:T(8,128)(2,1)S(1)} %copy-done), channel_id=1, source_target_pairs={{0,384},{128,0},{256,128},{384,256},{1,385},{129,1},{257,129},{385... | collective-permute-start | bytes 3145736 | tf_op jit(solution)/shard_map/ppermute | solution.py:26
  20.6 3.4 %collective-permute-start.10 = (bf16[1024,512]{1,0:T(8,128)(2,1)S(1)}, bf16[1024,512]{1,0:T(8,128)(2,1)}, u32[]{:S(2)}, u32[]{:S(2)}) collective-permute-start(bf16[1024,512]{1,0:T(8,128)(2,1)S(1)} %copy-done), channel_id=1, source_target_pairs={{0,256},{1,257},{128,384},{129,385},{256,0},{257,1},{384,128},{385... | collective-permute-start | bytes 3145736 | tf_op jit(solution)/shard_map/ppermute | solution.py:31
  24.0 2.9 %collective-permute-start.5 = (bf16[1024,512]{1,0:T(8,128)(2,1)S(1)}, bf16[1024,512]{1,0:T(8,128)(2,1)}, u32[]{:S(2)}, u32[]{:S(2)}) collective-permute-start(bf16[1024,512]{1,0:T(8,128)(2,1)S(1)} %copy-done), channel_id=1, source_target_pairs={{0,1},{1,0},{2,3},{3,2},{4,5},{5,4},{6,7},{7,6},{8,9},{9,8},{10,11... | collective-permute-start | bytes 3145736 | tf_op jit(solution)/shard_map/ppermute | solution.py:26
  26.9 14.9 %collective-permute-done.6.refs_8_.refs_6_ = bf16[1024,512]{1,0:T(8,128)(2,1)S(1)} collective-permute-done((bf16[1024,512]{1,0:T(8,128)(2,1)S(1)}, bf16[1024,512]{1,0:T(8,128)(2,1)S(1)}, u32[]{:S(2)}, u32[]{:S(2)}) %collective-permute-start.6) | collective-permute-done | bytes 1048608 | tf_op jit(solution)/shard_map/ppermute | solution.py:26
  41.8 2.9 %collective-permute-start.7 = (bf16[1024,512]{1,0:T(8,128)(2,1)S(1)}, bf16[1024,512]{1,0:T(8,128)(2,1)}, u32[]{:S(2)}, u32[]{:S(2)}) collective-permute-start(bf16[1024,512]{1,0:T(8,128)(2,1)S(1)} %collective-permute-done.6.refs_8_.refs_6_), channel_id=1, source_target_pairs={{0,1},{1,0},{2,3},{3,2},{4,5},{5,4},{6,7},{7,6},{8,9},{9,8},{10,11... | collective-permute-start | bytes 3145736 | tf_op jit(solution)/shard_map/ppermute | solution.py:26
  44.7 0.7 constant_dynamic-slice_fusion
  45.4 1.9 collective-permute-start
  47.3 0.0 collective-permute-done.8.refs_10_.refs_8_
  47.3 21.1 %collective-permute-start.9 = (bf16[1024,512]{1,0:T(8,128)(2,1)}, bf16[1024,512]{1,0:T(8,128)(2,1)}, u32[]{:S(2)}, u32[]{:S(2)}) collective-permute-start(bf16[1024,512]{1,0:T(8,128)(2,1)} %collective-permute-done.8.refs_10_.refs_8_), channel_id=1, source_target_pairs={{0,1},{1,0},{2,3},{3,2},{4,5},{5,4},{6,7},{7,6},{8,9},{9,8},{10,11... | collective-permute-start | bytes 3145736 | tf_op jit(solution)/shard_map/ppermute | solution.py:26
  68.4 0.0 collective-permute-done.10.refs_12_.refs_10_
  68.4 1.9 collective-permute-start.11
  70.3 0.1 pad_add_fusion.s_ref.refs_0_
  70.4 0.0 collective-permute-done.other_ref
  70.4 0.0 all-to-all-done.kv_ref
  70.4 5.4 %attend.1.refs_1_ = bf16[2,64,1024]{2,1,0:T(8,128)(2,1)S(1)} custom-call(s32[4]{0:T(128)S(1)} %pad_add_fusion.s_ref.refs_0_, s32[2]{0:T(128)S(1)} %copy-done.8, s32[64]{0:T(128)S(1)} %copy-done.7, bf16[128,1024]{1,0:T(8,128)(2,1)} %mine_ref.1, bf16[64,1024]{1,0:T(8,128)(2,1)S(1)} %collective-permute-done.other_ref, ...), custom_call_target="tpu_custom_call" | custom-call | tf_op jit(solution)/shard_map/attend/pallas_call | solution.py:95
  75.8 4.2 %collective-permute-start.3 = (bf16[2,64,1024]{2,1,0:T(8,128)(2,1)S(1)}, bf16[2,64,1024]{2,1,0:T(8,128)(2,1)S(1)}, u32[]{:S(2)}, u32[]{:S(2)}) collective-permute-start(bf16[2,64,1024]{2,1,0:T(8,128)(2,1)S(1)} %attend.1.refs_1_), channel_id=1, source_target_pairs={{0,32},{16,48},{32,64},{48,80},{64,96},{80,112},{96,0},{112,16},{1... | collective-permute-start | bytes 786440 | tf_op jit(solution)/shard_map/ppermute | solution.py:26
  80.1 10.8 %collective-permute-done.3.refs_4_ = bf16[2,64,1024]{2,1,0:T(8,128)(2,1)S(1)} collective-permute-done((bf16[2,64,1024]{2,1,0:T(8,128)(2,1)S(1)}, bf16[2,64,1024]{2,1,0:T(8,128)(2,1)S(1)}, u32[]{:S(2)}, u32[]{:S(2)}) %collective-permute-start.3) | collective-permute-done | bytes 262176 | tf_op jit(solution)/shard_map/ppermute | solution.py:26
  90.9 3.1 %collective-permute-start.4 = (bf16[2,64,1024]{2,1,0:T(8,128)(2,1)S(1)}, bf16[2,64,1024]{2,1,0:T(8,128)(2,1)S(1)}, u32[]{:S(2)}, u32[]{:S(2)}) collective-permute-start(bf16[2,64,1024]{2,1,0:T(8,128)(2,1)S(1)} %attend.1.refs_1_), channel_id=1, source_target_pairs={{0,96},{16,112},{32,0},{48,16},{64,32},{80,48},{96,64},{112,80},{1... | collective-permute-start | bytes 786440 | tf_op jit(solution)/shard_map/ppermute | solution.py:26
  94.0 5.5 %collective-permute-done.4.refs_5_ = bf16[2,64,1024]{2,1,0:T(8,128)(2,1)S(1)} collective-permute-done((bf16[2,64,1024]{2,1,0:T(8,128)(2,1)S(1)}, bf16[2,64,1024]{2,1,0:T(8,128)(2,1)S(1)}, u32[]{:S(2)}, u32[]{:S(2)}) %collective-permute-start.4) | collective-permute-done | bytes 262176 | tf_op jit(solution)/shard_map/ppermute | solution.py:26
  99.5 9.2 %collective-permute-start.12 = (bf16[2,64,1024]{2,1,0:T(8,128)(2,1)S(1)}, bf16[2,64,1024]{2,1,0:T(8,128)(2,1)S(1)}, u32[]{:S(2)}, u32[]{:S(2)}) collective-permute-start(bf16[2,64,1024]{2,1,0:T(8,128)(2,1)S(1)} %collective-permute-done.3.refs_4_), channel_id=1, source_target_pairs={{0,16},{16,32},{32,48},{48,64},{64,80},{80,96},{96,112},{112,0},{1... | collective-permute-start | bytes 786440 | tf_op jit(solution)/shard_map/ppermute | solution.py:26
  108.8 0.0 collective-permute-done.5.refs_7_.refs_5_
  108.8 4.2 %collective-permute-start.13 = (bf16[2,64,1024]{2,1,0:T(8,128)(2,1)S(1)}, bf16[2,64,1024]{2,1,0:T(8,128)(2,1)S(1)}, u32[]{:S(2)}, u32[]{:S(2)}) collective-permute-start(bf16[2,64,1024]{2,1,0:T(8,128)(2,1)S(1)} %collective-permute-done.4.refs_5_), channel_id=1, source_target_pairs={{0,112},{16,0},{32,16},{48,32},{64,48},{80,64},{96,80},{112,96},{1... | collective-permute-start | bytes 786440 | tf_op jit(solution)/shard_map/ppermute | solution.py:26
  113.0 0.0 collective-permute-done.7.refs_9_.refs_7_
  113.0 5.1 %collective-permute-start.14 = (bf16[2,64,1024]{2,1,0:T(8,128)(2,1)S(1)}, bf16[2,64,1024]{2,1,0:T(8,128)(2,1)S(1)}, u32[]{:S(2)}, u32[]{:S(2)}) collective-permute-start(bf16[2,64,1024]{2,1,0:T(8,128)(2,1)S(1)} %broadcast_select_fusion), channel_id=1, source_target_pairs={{0,32},{1,97},{16,48},{17,113},{32,64},{33,1},{48,80},{49,17},{64,... | collective-permute-start | bytes 786440 | tf_op jit(solution)/shard_map/ppermute | solution.py:31
  118.1 0.0 collective-permute-done.9.refs_11_.refs_9_
  118.1 0.0 collective-permute-done.11.refs_13_.refs_11_
  118.1 3.5 %collective-permute-done.13.refs_2_ = bf16[2,64,1024]{2,1,0:T(8,128)(2,1)S(1)} collective-permute-done((bf16[2,64,1024]{2,1,0:T(8,128)(2,1)S(1)}, bf16[2,64,1024]{2,1,0:T(8,128)(2,1)S(1)}, u32[]{:S(2)}, u32[]{:S(2)}) %collective-permute-start.13) | collective-permute-done | bytes 262176 | tf_op jit(solution)/shard_map/ppermute | solution.py:26
  121.6 8.1 %collective-permute-done.14.refs_3_ = bf16[2,64,1024]{2,1,0:T(8,128)(2,1)S(1)} collective-permute-done((bf16[2,64,1024]{2,1,0:T(8,128)(2,1)S(1)}, bf16[2,64,1024]{2,1,0:T(8,128)(2,1)S(1)}, u32[]{:S(2)}, u32[]{:S(2)}) %collective-permute-start.14) | collective-permute-done | bytes 262176 | tf_op jit(solution)/shard_map/ppermute | solution.py:31
  129.8 5.7 %project.3 = bf16[8,4,32,384]{3,2,1,0:T(8,128)(2,1)} custom-call(s32[4]{0:T(128)S(1)} %pad_add_fusion.s_ref.refs_0_, bf16[2,64,1024]{2,1,0:T(8,128)(2,1)S(1)} %collective-permute-done.12.refs_1_, bf16[2,64,1024]{2,1,0:T(8,128)(2,1)S(1)} %collective-permute-done.13.refs_2_, bf16[2,64,1024]{2,1,0:T(8,128)(2,1)S(1)} %collective-permute-done.14.refs_3_, ...), custom_call_target="tpu_custom_call" | custom-call | tf_op jit(solution)/shard_map/project/pallas_call | solution.py:131
  135.5 10.3 %all-to-all-start.2 = ((bf16[32,32,384]{2,1,0:T(8,128)(2,1)}), bf16[32,32,384]{2,1,0:T(8,128)(2,1)}, u32[]{:S(2)}, u32[]{:S(2)}) async-start(bf16[32,32,384]{2,1,0:T(8,128)(2,1)} %bitcast.7), calls=%async_computation.2 | async-start | bytes 1572864 | tf_op jit(solution)/shard_map/all_to_all | solution.py:208
  145.7 1.9 collective-permute-start.1
  147.7 4.6 %collective-permute-start.2 = (bf16[2,64,1024]{2,1,0:T(8,128)(2,1)S(1)}, bf16[2,64,1024]{2,1,0:T(8,128)(2,1)S(1)}, u32[]{:S(2)}, u32[]{:S(2)}) collective-permute-start(bf16[2,64,1024]{2,1,0:T(8,128)(2,1)S(1)} %attend.1.refs_1_), channel_id=1, source_target_pairs={{0,112},{16,0},{32,16},{48,32},{64,48},{80,64},{96,80},{112,96},{1... | collective-permute-start | bytes 786440 | tf_op jit(solution)/shard_map/ppermute | solution.py:26
  152.3 4.1 %collective-permute-done.1.refs_2_ = bf16[2,64,1024]{2,1,0:T(8,128)(2,1)S(1)} collective-permute-done((bf16[2,64,1024]{2,1,0:T(8,128)(2,1)S(1)}, bf16[2,64,1024]{2,1,0:T(8,128)(2,1)S(1)}, u32[]{:S(2)}, u32[]{:S(2)}) %collective-permute-start.1) | collective-permute-done | bytes 262176 | tf_op jit(solution)/shard_map/ppermute | solution.py:26
  156.3 2.8 %collective-permute-done.2.refs_3_ = bf16[2,64,1024]{2,1,0:T(8,128)(2,1)S(1)} collective-permute-done((bf16[2,64,1024]{2,1,0:T(8,128)(2,1)S(1)}, bf16[2,64,1024]{2,1,0:T(8,128)(2,1)S(1)}, u32[]{:S(2)}, u32[]{:S(2)}) %collective-permute-start.2) | collective-permute-done | bytes 262176 | tf_op jit(solution)/shard_map/ppermute | solution.py:26
  159.2 0.9 copy-done.2
  160.1 0.9 copy-done.4
  161.1 0.9 copy-done.6
  162.0 5.9 %project.2 = bf16[8,4,32,640]{3,2,1,0:T(8,128)(2,1)S(1)} custom-call(s32[4]{0:T(128)S(1)} %pad_add_fusion.s_ref.refs_0_, bf16[2,64,1024]{2,1,0:T(8,128)(2,1)S(1)} %copy-done.2, bf16[2,64,1024]{2,1,0:T(8,128)(2,1)S(1)} %collective-permute-done.1.refs_2_, bf16[2,64,1024]{2,1,0:T(8,128)(2,1)S(1)} %collective-permute-done.2.refs_3_, ...), custom_call_target="tpu_custom_call" | custom-call | tf_op jit(solution)/shard_map/project/pallas_call | solution.py:131
  167.9 0.0 copy-start.9
  167.9 0.0 copy-start.10
  168.0 44.1 %all_to_all.20 = bf16[32,32,640]{2,1,0:T(8,128)(2,1)S(1)} all-to-all(bf16[32,32,640]{2,1,0:T(8,128)(2,1)S(1)} %bitcast.10), channel_id=1, replica_groups=mesh['x'=4,'y'=8,'z'=8,'c'=2] {'z','x'}, dimensions={0} | all-to-all | bytes 2621440 | tf_op jit(solution)/shard_map/all_to_all | solution.py:208
  212.1 1.8 place.1
  213.9 18.3 %all_to_all.21.i_ref = bf16[16,32,384]{2,1,0:T(8,128)(2,1)S(1)} all-to-all(bf16[16,32,384]{2,1,0:T(8,128)(2,1)S(1)} %place.1), channel_id=1, replica_groups=mesh['x'=4,'y'=8,'z'=8,'c'=2] {'z','c'}, dimensions={0} | all-to-all | bytes 786432 | tf_op jit(solution)/shard_map/all_to_all | solution.py:208
  232.2 0.9 finish.1
  (21 shorter events, 0.1 us)
Async XLA Ops:
  2.1 12.0 %copy-start = (bf16[1024,512]{1,0:T(8,128)(2,1)S(1)}, bf16[1024,512]{1,0:T(8,128)(2,1)}, u32[]{:S(2)}) copy-start(bf16[1024,512]{1,0:T(8,128)(2,1)} %refs_4_.1) | copy-start | bytes 3145732
  2.1 42.6 %copy-start.11 = (bf16[128,1024]{1,0:T(8,128)(2,1)S(1)}, bf16[128,1024]{1,0:T(8,128)(2,1)}, u32[]{:S(2)}) copy-start(bf16[128,1024]{1,0:T(8,128)(2,1)} %mine_ref.1) | copy-start | bytes 786436
  2.1 68.3 %copy-start.7 = (s32[64]{0:T(128)S(1)}, s32[64]{0:T(128)}, u32[]{:S(2)}) copy-start(s32[64]{0:T(128)} %length_ref.1) | copy-start | bytes 772
  2.1 68.3 %copy-start.8 = (s32[2]{0:T(128)S(1)}, s32[2]{0:T(128)}, u32[]{:S(2)}) copy-start(s32[2]{0:T(128)} %cache_ref.1) | copy-start | bytes 28
  2.1 68.3 %all-to-all-start = ((bf16[16,2,128,128]{3,2,1,0:T(8,128)(2,1)}), bf16[16,2,128,128]{3,2,1,0:T(8,128)(2,1)S(1)}, u32[]{:S(2)}, u32[]{:S(2)}) async-start(bf16[16,2,128,128]{3,2,1,0:T(8,128)(2,1)} %bitcast.4), calls=%async_computation | async-start | bytes 2097152 | tf_op jit(solution)/shard_map/all_to_all | solution.py:208
  14.1 27.7 %collective-permute-start.6 = (bf16[1024,512]{1,0:T(8,128)(2,1)S(1)}, bf16[1024,512]{1,0:T(8,128)(2,1)S(1)}, u32[]{:S(2)}, u32[]{:S(2)}) collective-permute-start(bf16[1024,512]{1,0:T(8,128)(2,1)S(1)} %copy-done), channel_id=1, source_target_pairs={{0,128},{128,256},{256,384},{384,0},{1,129},{129,257},{257,385},{3... | collective-permute-start | bytes 3145736 | tf_op jit(solution)/shard_map/ppermute | solution.py:26
  17.2 30.1 %collective-permute-start.8 = (bf16[1024,512]{1,0:T(8,128)(2,1)S(1)}, bf16[1024,512]{1,0:T(8,128)(2,1)}, u32[]{:S(2)}, u32[]{:S(2)}) collective-permute-start(bf16[1024,512]{1,0:T(8,128)(2,1)S(1)} %copy-done), channel_id=1, source_target_pairs={{0,384},{128,0},{256,128},{384,256},{1,385},{129,1},{257,129},{385... | collective-permute-start | bytes 3145736 | tf_op jit(solution)/shard_map/ppermute | solution.py:26
  20.6 47.8 %collective-permute-start.10 = (bf16[1024,512]{1,0:T(8,128)(2,1)S(1)}, bf16[1024,512]{1,0:T(8,128)(2,1)}, u32[]{:S(2)}, u32[]{:S(2)}) collective-permute-start(bf16[1024,512]{1,0:T(8,128)(2,1)S(1)} %copy-done), channel_id=1, source_target_pairs={{0,256},{1,257},{128,384},{129,385},{256,0},{257,1},{384,128},{385... | collective-permute-start | bytes 3145736 | tf_op jit(solution)/shard_map/ppermute | solution.py:31
  24.0 84.7 %collective-permute-start.5 = (bf16[1024,512]{1,0:T(8,128)(2,1)S(1)}, bf16[1024,512]{1,0:T(8,128)(2,1)}, u32[]{:S(2)}, u32[]{:S(2)}) collective-permute-start(bf16[1024,512]{1,0:T(8,128)(2,1)S(1)} %copy-done), channel_id=1, source_target_pairs={{0,1},{1,0},{2,3},{3,2},{4,5},{5,4},{6,7},{7,6},{8,9},{9,8},{10,11... | collective-permute-start | bytes 3145736 | tf_op jit(solution)/shard_map/ppermute | solution.py:26
  41.8 71.2 %collective-permute-start.7 = (bf16[1024,512]{1,0:T(8,128)(2,1)S(1)}, bf16[1024,512]{1,0:T(8,128)(2,1)}, u32[]{:S(2)}, u32[]{:S(2)}) collective-permute-start(bf16[1024,512]{1,0:T(8,128)(2,1)S(1)} %collective-permute-done.6.refs_8_.refs_6_), channel_id=1, source_target_pairs={{0,1},{1,0},{2,3},{3,2},{4,5},{5,4},{6,7},{7,6},{8,9},{9,8},{10,11... | collective-permute-start | bytes 3145736 | tf_op jit(solution)/shard_map/ppermute | solution.py:26
  45.4 25.0 %collective-permute-start = (bf16[64,1024]{1,0:T(8,128)(2,1)}, bf16[64,1024]{1,0:T(8,128)(2,1)S(1)}, u32[]{:S(2)}, u32[]{:S(2)}) collective-permute-start(bf16[64,1024]{1,0:T(8,128)(2,1)} %constant_dynamic-slice_fusion), channel_id=1, source_target_pairs={{0,1},{1,0},{2,3},{3,2},{4,5},{5,4},{6,7},{7,6},{8,9},{9,8},{10,11... | collective-permute-start | bytes 393224 | tf_op jit(solution)/shard_map/ppermute | solution.py:26
  47.3 70.8 %collective-permute-start.9 = (bf16[1024,512]{1,0:T(8,128)(2,1)}, bf16[1024,512]{1,0:T(8,128)(2,1)}, u32[]{:S(2)}, u32[]{:S(2)}) collective-permute-start(bf16[1024,512]{1,0:T(8,128)(2,1)} %collective-permute-done.8.refs_10_.refs_8_), channel_id=1, source_target_pairs={{0,1},{1,0},{2,3},{3,2},{4,5},{5,4},{6,7},{7,6},{8,9},{9,8},{10,11... | collective-permute-start | bytes 3145736 | tf_op jit(solution)/shard_map/ppermute | solution.py:26
  68.4 49.7 %collective-permute-start.11 = (bf16[1024,512]{1,0:T(8,128)(2,1)}, bf16[1024,512]{1,0:T(8,128)(2,1)}, u32[]{:S(2)}, u32[]{:S(2)}) collective-permute-start(bf16[1024,512]{1,0:T(8,128)(2,1)} %collective-permute-done.10.refs_12_.refs_10_), channel_id=1, source_target_pairs={{0,1},{1,0},{2,3},{3,2},{4,5},{5,4},{6,7},{7,6},{8,9},{9,8},{10,11... | collective-permute-start | bytes 3145736 | tf_op jit(solution)/shard_map/ppermute | solution.py:26
  75.8 71.8 %copy-start.1 = (bf16[2,64,1024]{2,1,0:T(8,128)(2,1)}, bf16[2,64,1024]{2,1,0:T(8,128)(2,1)S(1)}, u32[]{:S(2)}) copy-start(bf16[2,64,1024]{2,1,0:T(8,128)(2,1)S(1)} %attend.1.refs_1_) | copy-start | bytes 786436
  75.8 15.0 %collective-permute-start.3 = (bf16[2,64,1024]{2,1,0:T(8,128)(2,1)S(1)}, bf16[2,64,1024]{2,1,0:T(8,128)(2,1)S(1)}, u32[]{:S(2)}, u32[]{:S(2)}) collective-permute-start(bf16[2,64,1024]{2,1,0:T(8,128)(2,1)S(1)} %attend.1.refs_1_), channel_id=1, source_target_pairs={{0,32},{16,48},{32,64},{48,80},{64,96},{80,112},{96,0},{112,16},{1... | collective-permute-start | bytes 786440 | tf_op jit(solution)/shard_map/ppermute | solution.py:26
  90.9 44.6 %copy-start.3 = (bf16[2,64,1024]{2,1,0:T(8,128)(2,1)}, bf16[2,64,1024]{2,1,0:T(8,128)(2,1)S(1)}, u32[]{:S(2)}) copy-start(bf16[2,64,1024]{2,1,0:T(8,128)(2,1)S(1)} %collective-permute-done.3.refs_4_) | copy-start | bytes 786436
  90.9 8.6 %collective-permute-start.4 = (bf16[2,64,1024]{2,1,0:T(8,128)(2,1)S(1)}, bf16[2,64,1024]{2,1,0:T(8,128)(2,1)S(1)}, u32[]{:S(2)}, u32[]{:S(2)}) collective-permute-start(bf16[2,64,1024]{2,1,0:T(8,128)(2,1)S(1)} %attend.1.refs_1_), channel_id=1, source_target_pairs={{0,96},{16,112},{32,0},{48,16},{64,32},{80,48},{96,64},{112,80},{1... | collective-permute-start | bytes 786440 | tf_op jit(solution)/shard_map/ppermute | solution.py:26
  99.5 36.0 %copy-start.5 = (bf16[2,64,1024]{2,1,0:T(8,128)(2,1)}, bf16[2,64,1024]{2,1,0:T(8,128)(2,1)S(1)}, u32[]{:S(2)}) copy-start(bf16[2,64,1024]{2,1,0:T(8,128)(2,1)S(1)} %collective-permute-done.4.refs_5_) | copy-start | bytes 786436
  99.5 18.6 %collective-permute-start.12 = (bf16[2,64,1024]{2,1,0:T(8,128)(2,1)S(1)}, bf16[2,64,1024]{2,1,0:T(8,128)(2,1)S(1)}, u32[]{:S(2)}, u32[]{:S(2)}) collective-permute-start(bf16[2,64,1024]{2,1,0:T(8,128)(2,1)S(1)} %collective-permute-done.3.refs_4_), channel_id=1, source_target_pairs={{0,16},{16,32},{32,48},{48,64},{64,80},{80,96},{96,112},{112,0},{1... | collective-permute-start | bytes 786440 | tf_op jit(solution)/shard_map/ppermute | solution.py:26
  108.8 12.9 %collective-permute-start.13 = (bf16[2,64,1024]{2,1,0:T(8,128)(2,1)S(1)}, bf16[2,64,1024]{2,1,0:T(8,128)(2,1)S(1)}, u32[]{:S(2)}, u32[]{:S(2)}) collective-permute-start(bf16[2,64,1024]{2,1,0:T(8,128)(2,1)S(1)} %collective-permute-done.4.refs_5_), channel_id=1, source_target_pairs={{0,112},{16,0},{32,16},{48,32},{64,48},{80,64},{96,80},{112,96},{1... | collective-permute-start | bytes 786440 | tf_op jit(solution)/shard_map/ppermute | solution.py:26
  113.0 16.8 %collective-permute-start.14 = (bf16[2,64,1024]{2,1,0:T(8,128)(2,1)S(1)}, bf16[2,64,1024]{2,1,0:T(8,128)(2,1)S(1)}, u32[]{:S(2)}, u32[]{:S(2)}) collective-permute-start(bf16[2,64,1024]{2,1,0:T(8,128)(2,1)S(1)} %broadcast_select_fusion), channel_id=1, source_target_pairs={{0,32},{1,97},{16,48},{17,113},{32,64},{33,1},{48,80},{49,17},{64,... | collective-permute-start | bytes 786440 | tf_op jit(solution)/shard_map/ppermute | solution.py:31
  135.5 32.4 %all-to-all-start.2 = ((bf16[32,32,384]{2,1,0:T(8,128)(2,1)}), bf16[32,32,384]{2,1,0:T(8,128)(2,1)}, u32[]{:S(2)}, u32[]{:S(2)}) async-start(bf16[32,32,384]{2,1,0:T(8,128)(2,1)} %bitcast.7), calls=%async_computation.2 | async-start | bytes 1572864 | tf_op jit(solution)/shard_map/all_to_all | solution.py:208
  145.7 10.6 %collective-permute-start.1 = (bf16[2,64,1024]{2,1,0:T(8,128)(2,1)S(1)}, bf16[2,64,1024]{2,1,0:T(8,128)(2,1)S(1)}, u32[]{:S(2)}, u32[]{:S(2)}) collective-permute-start(bf16[2,64,1024]{2,1,0:T(8,128)(2,1)S(1)} %attend.1.refs_1_), channel_id=1, source_target_pairs={{0,16},{16,32},{32,48},{48,64},{64,80},{80,96},{96,112},{112,0},{1... | collective-permute-start | bytes 786440 | tf_op jit(solution)/shard_map/ppermute | solution.py:26
  147.7 11.5 %collective-permute-start.2 = (bf16[2,64,1024]{2,1,0:T(8,128)(2,1)S(1)}, bf16[2,64,1024]{2,1,0:T(8,128)(2,1)S(1)}, u32[]{:S(2)}, u32[]{:S(2)}) collective-permute-start(bf16[2,64,1024]{2,1,0:T(8,128)(2,1)S(1)} %attend.1.refs_1_), channel_id=1, source_target_pairs={{0,112},{16,0},{32,16},{48,32},{64,48},{80,64},{96,80},{112,96},{1... | collective-permute-start | bytes 786440 | tf_op jit(solution)/shard_map/ppermute | solution.py:26
  159.2 1.0 copy-start.2
  160.1 0.9 copy-start.4
  161.1 0.9 copy-start.6
  167.9 44.2 %copy-start.9 = (s32[64]{0:T(128)S(1)}, s32[64]{0:T(128)}, u32[]{:S(2)}) copy-start(s32[64]{0:T(128)} %group_ref.1) | copy-start | bytes 772
  167.9 44.2 %copy-start.10 = (s32[64]{0:T(128)S(1)}, s32[64]{0:T(128)}, u32[]{:S(2)}) copy-start(s32[64]{0:T(128)} %first_ref.1) | copy-start | bytes 772
